TPU v7x, 8 devices: a whole 2x2x1 slice. The times are simulated.
8 devices in a mesh: rep: 1 (over z), r: 2 (over y), s: 4 (over x, core).
Axes of the slice: x: 2, y: 2, z: 1, core: 2. Of those that a mesh axis runs over, the one named last changes fastest.
Arguments:
- x: bfloat16 [8, 4096, 1024], P(('rep', 'r', 's'))
- dy: bfloat16 [8, 4096, 1024], P(('rep', 'r', 's'))
- w_gate: bfloat16 [2, 1024, 2816], P(None, 's')
- w_up: bfloat16 [2, 1024, 2816], P(None, 's')
- w_down: bfloat16 [2, 2816, 1024], P(None, 's')
- m_w_gate: float32 [2, 1024, 2816], P(None, 's')
- m_w_up: float32 [2, 1024, 2816], P(None, 's')
- m_w_down: float32 [2, 2816, 1024], P(None, 's')
- v_w_gate: float32 [2, 1024, 2816], P(None, 's')
- v_w_up: float32 [2, 1024, 2816], P(None, 's')
- v_w_down: float32 [2, 2816, 1024], P(None, 's')
Outputs:
- output 1: bfloat16 [2, 1024, 2816], P('rep', 's')
- output 2: bfloat16 [2, 1024, 2816], P('rep', 's')
- output 3: bfloat16 [2, 2816, 1024], P('rep', 's')
- output 4: float32 [2, 1024, 2816], P('rep', 's')
- output 5: float32 [2, 1024, 2816], P('rep', 's')
- output 6: float32 [2, 2816, 1024], P('rep', 's')
- output 7: float32 [2, 1024, 2816], P('rep', 's')
- output 8: float32 [2, 1024, 2816], P('rep', 's')
- output 9: float32 [2, 2816, 1024], P('rep', 's')
All inputs are finite; a program needn't handle non-finite values.
Results may differ from a plain program's by a relative error of at most 0.022.
Values are sent between devices in bfloat16 or wider.
A program may use at most 2 GiB of HBM per device.

v0:
```python
import jax
import jax.numpy as jnp
from jax import lax
from jax.sharding import PartitionSpec as P

NAMES = ("w_gate", "w_up", "w_down")


def matmul(a, w):
    return jnp.dot(a, w, preferred_element_type=jnp.float32).astype(jnp.bfloat16)


def normed(h):
    wide = h.astype(jnp.float32)
    scale = lax.rsqrt(jnp.mean(wide**2, -1, keepdims=True) + 1e-6)
    return (wide * scale).astype(jnp.bfloat16)


def layer(h, w):
    a = normed(h)
    gate = jnp.dot(a, w["w_gate"], preferred_element_type=jnp.float32)
    up = jnp.dot(a, w["w_up"], preferred_element_type=jnp.float32)
    return h + matmul((jax.nn.silu(gate) * up).astype(jnp.bfloat16), w["w_down"])


def adamw(w, m, v, g):
    m = 0.9 * m + 0.1 * g
    v = 0.95 * v + 0.05 * g * g
    step = m * lax.rsqrt(v + 1e-8) + 0.1 * w
    return (w - 0.02 * step).astype(jnp.bfloat16), m, v


def clipped(gradients, sum_of_squares, count):
    factor = jnp.minimum(1.0, 0.5 * lax.rsqrt(sum_of_squares / count + 1e-30))
    return [g * factor for g in gradients]


def solution(mesh):
    def fetched(weights, number):
        return {name: lax.all_gather(w[number], "s", axis=0, tiled=True) for name, w in zip(NAMES, weights, strict=True)}

    def summed(term):
        return lax.psum(lax.psum_scatter(term, "s", scatter_dimension=0, tiled=True), "r")

    def step(x, dy, *arrays):
        weights, m, v = (arrays[i : i + 3] for i in (0, 3, 6))
        layers = weights[0].shape[0]
        h, kept = x[0], []
        for number in range(layers):
            kept.append(h)
            h = layer(h, fetched(weights, number))
        by_h, mine = dy[0], [None] * layers
        for number in reversed(range(layers)):
            _, back = jax.vjp(lambda w, h: layer(h, w), fetched(weights, number), kept[number])
            by_w, by_h = back(by_h)
            mine[number] = [summed(by_w[name]) for name in NAMES]
        gradients = [jnp.stack([mine[number][i] for number in range(layers)]).astype(jnp.float32) for i in range(3)]
        squares = lax.psum(sum(jnp.sum(g * g) for g in gradients), "s")
        gradients = clipped(gradients, squares, lax.psum(1, "s") * sum(g.size for g in gradients))
        new = [adamw(w.astype(jnp.float32), m, v, g) for w, m, v, g in zip(weights, m, v, gradients, strict=True)]
        return tuple(one[which] for which in range(3) for one in new)

    states, cut = P(("rep", "r", "s"), None, None), P(None, "s", None)
    return jax.shard_map(
        step,
        mesh=mesh,
        in_specs=(states, states) + (cut,) * 9,
        out_specs=(P("rep", "s", None),) * 9,
        check_vma=False,
    )
```

profile of v0, /device:TPU:0, one launch (start us, length us, event | category | flops | bytes accessed | tf_op | source)
XLA Modules:
  0.0 1019.0 jit_solution(475931790214713648)
XLA Ops:
  18.3 12.0 %copy.20 = bf16[1,4096,1024]{1,2,0:T(8,128)(2,1)} copy(bf16[1,4096,1024]{2,1,0:T(8,128)(2,1)} %param.11) | data formatting | bytes 16777216 | tf_op args[0]
  35.4 11.3 %copy.21 = bf16[1,4096,1024]{1,2,0:T(8,128)(2,1)} copy(bf16[1,4096,1024]{2,1,0:T(8,128)(2,1)} %param.12) | data formatting | bytes 16777216 | tf_op args[1]
  54.5 32.4 %fusion.59 = f32[4096,2816]{1,0:T(8,128)} fusion(bf16[1,1024,2816]{2,1,0:T(8,128)(2,1)} %all-gather.13.cloned.1.call-done, bf16[1,4096,1024]{1,2,0:T(8,128)(2,1)} %copy.20, f32[4096]{0:T(1024)S(1)} %add_rsqrt_fusion), kind=kOutput, calls=%fused_computation.93 | convolution fusion | flops 23634903040 | bytes 60309504 | tf_op jit(solution)/shard_map/dot_general | solution.py:21
  86.9 10.4 %all-gather.15.cloned.1.call-done = bf16[1,1024,2816]{2,1,0:T(8,128)(2,1)} async-done(((bf16[1,256,2816]{2,1,0:T(8,128)(2,1)}), bf16[1,1024,2816]{2,1,0:T(8,128)(2,1)}) %all-gather.15.cloned.1.call-update) | async-done | bytes 5767184 | tf_op jit(solution)/shard_map/all_gather | solution.py:40
  97.3 54.8 %multiply_convert_fusion.1 = (bf16[4096,2816]{1,0:T(8,128)(2,1)}, f32[4096,2816]{1,0:T(8,128)}) fusion(f32[4096,2816]{1,0:T(8,128)} %fusion.59, bf16[1,1024,2816]{2,1,0:T(8,128)(2,1)} %all-gather.15.cloned.1.call-done, bf16[1,4096,1024]{1,2,0:T(8,128)(2,1)} %copy.20, f32[4096]{0:T(1024)S(1)} %add_rsqrt_fusion), kind=kOutput, calls=%fused_computation.17 | convolution fusion | flops 23704109056 | bytes 129515520 | tf_op jit(solution)/shard_map/dot_general | solution.py:22
  152.1 32.7 %fusion.19 = (f32[4096]{0:T(1024)S(1)}, bf16[4096,1024]{0,1:T(8,128)(2,1)}) fusion(bf16[4096,2816]{1,0:T(8,128)(2,1)} %get-tuple-element.30, bf16[1,2816,1024]{2,1,0:T(8,128)(2,1)} %all-gather.17.cloned.1.call-done, bf16[1,4096,1024]{1,2,0:T(8,128)(2,1)} %copy.20), kind=kOutput, calls=%fused_computation.37 | convolution fusion | flops 23643287552 | bytes 45629440 | tf_op jit(solution)/shard_map/dot_general | solution.py:10
  184.8 31.7 %convolution_convert_fusion.1 = bf16[4096,2816]{1,0:T(8,128)(2,1)} fusion(bf16[1,4096,1024]{2,1,0:T(8,128)(2,1)} %param.12, bf16[1,2816,1024]{2,1,0:T(8,128)(2,1)} %all-gather.21.cloned.1.call-done), kind=kOutput, calls=%fused_computation.29 | convolution fusion | flops 23633854464 | bytes 37224448 | tf_op jit(solution)/shard_map/transpose(jvp())/dot_general | solution.py:10
  225.1 32.5 %fusion.47 = f32[4096,2816]{1,0:T(8,128)} fusion(bf16[1,1024,2816]{2,1,0:T(8,128)(2,1)} %all-gather.23.cloned.1.call-done, bf16[4096,1024]{0,1:T(8,128)(2,1)} %get-tuple-element.33, f32[4096]{0:T(1024)S(1)} %fusion.77), kind=kOutput, calls=%fused_computation.81 | convolution fusion | flops 23634903040 | bytes 60309504 | tf_op jit(solution)/shard_map/jvp()/dot_general | solution.py:22
  267.7 62.4 %fusion.2 = (bf16[4096,2816]{1,0:T(8,128)(2,1)}, f32[4096,2816]{1,0:T(8,128)}) fusion(f32[4096,2816]{1,0:T(8,128)} %fusion.47, bf16[4096,2816]{1,0:T(8,128)(2,1)} %convolution_convert_fusion.1, bf16[1,1024,2816]{2,1,0:T(8,128)(2,1)} %all-gather.19.cloned.1.call-done, bf16[4096,1024]{0,1:T(8,128)(2,1)} %get-tuple-element.33, f32[4096]{0:T(1024)S(1)} %fusion.77), kind=kOutput, calls=%fused_computation.8 | convolution fusion | flops 23773315072 | bytes 152584192 | tf_op jit(solution)/shard_map/jvp()/dot_general | solution.py:21
  330.1 28.8 %fusion.51 = bf16[4096,1024]{0,1:T(8,128)(2,1)} fusion(bf16[4096,2816]{1,0:T(8,128)(2,1)} %get-tuple-element.34, bf16[1,1024,2816]{2,1,0:T(8,128)(2,1)S(1)} %copy-done.14), kind=kOutput, calls=%fused_computation.85 | convolution fusion | flops 23622320128 | bytes 37224448 | tf_op jit(solution)/shard_map/transpose(jvp())/dot_general | solution.py:21
  358.9 42.3 %fusion.21 = (f32[4096]{0:T(1024)S(1)}, bf16[4096,1024]{0,1:T(8,128)(2,1)}) fusion(bf16[4096,1024]{0,1:T(8,128)(2,1)} %get-tuple-element.33, bf16[4096,1024]{0,1:T(8,128)(2,1)} %fusion.51, bf16[1,1024,2816]{2,1,0:T(8,128)(2,1)} %all-gather.23.cloned.1.call-done, bf16[4096,2816]{1,0:T(8,128)(2,1)} %convolution_convert_fusion.1, ...), kind=kOutput, calls=%fused_computation.39 | convolution fusion | flops 23716687872 | bytes 100155392 | tf_op jit(solution)/shard_map/transpose(jvp())/dot_general | solution.py:22
  401.2 13.8 %fusion.22 = bf16[4096,1024]{0,1:T(8,128)(2,1)} fusion(bf16[4096,1024]{0,1:T(8,128)(2,1)} %get-tuple-element.33, bf16[4096,1024]{0,1:T(8,128)(2,1)} %get-tuple-element.37, bf16[1,4096,1024]{1,2,0:T(8,128)(2,1)} %copy.21, f32[4096]{0:T(1024)S(1)} %multiply_multiply_fusion.3, f32[4096]{0:T(1024)S(1)} %fusion.77), kind=kLoop, calls=%fused_computation.43 | loop fusion | flops 29360128 | bytes 33587200 | tf_op jit(solution)/shard_map/transpose(jvp())/add_any | solution.py:14
  415.0 33.3 %convolution_convert_fusion.2 = bf16[2816,1024]{1,0:T(8,128)(2,1)} fusion(bf16[4096,2816]{1,0:T(8,128)(2,1)} %get-tuple-element.30, bf16[4096,1024]{0,1:T(8,128)(2,1)} %fusion.22), kind=kOutput, calls=%fused_computation.99 | convolution fusion | flops 23625203712 | bytes 37224448 | tf_op jit(solution)/shard_map/transpose(jvp())/dot_general | solution.py:10
  448.4 41.1 %fusion.61 = bf16[2816,1024]{1,0:T(8,128)(2,1)} fusion(bf16[1,4096,1024]{2,1,0:T(8,128)(2,1)} %param.12, f32[4096,2816]{1,0:T(8,128)} %fusion.47, f32[4096,2816]{1,0:T(8,128)} %get-tuple-element.35), kind=kOutput, calls=%fused_computation.95 | convolution fusion | flops 23694409728 | bytes 106430464 | tf_op jit(solution)/shard_map/transpose(jvp())/dot_general | solution.py:10
  489.6 30.7 %convolution_convert_fusion = bf16[4096,2816]{1,0:T(8,128)(2,1)} fusion(bf16[4096,1024]{0,1:T(8,128)(2,1)} %fusion.22, bf16[1,2816,1024]{2,1,0:T(8,128)(2,1)} %all-gather.17.cloned.1.call-done), kind=kOutput, calls=%fused_computation.28 | convolution fusion | flops 23633854464 | bytes 37224448 | tf_op jit(solution)/shard_map/transpose(jvp())/dot_general | solution.py:10
  520.3 36.8 %fusion.68 = bf16[1024,2816]{1,0:T(8,128)(2,1)} fusion(bf16[4096,2816]{1,0:T(8,128)(2,1)} %convolution_convert_fusion, f32[4096,2816]{1,0:T(8,128)} %fusion.59, bf16[1,4096,1024]{1,2,0:T(8,128)(2,1)} %copy.20, f32[4096]{0:T(1024)S(1)} %copy-done.13), kind=kOutput, calls=%fused_computation.98 | convolution fusion | flops 23706992640 | bytes 83378176 | tf_op jit(solution)/shard_map/transpose(jvp())/dot_general | solution.py:22
  557.1 36.6 %fusion.64 = bf16[1024,2816]{1,0:T(8,128)(2,1)} fusion(bf16[4096,2816]{1,0:T(8,128)(2,1)} %convolution_convert_fusion.1, bf16[4096,1024]{0,1:T(8,128)(2,1)} %get-tuple-element.33, f32[4096]{0:T(1024)S(1)} %copy-done.9, f32[4096,2816]{1,0:T(8,128)} %get-tuple-element.35), kind=kOutput, calls=%fused_computation.96 | convolution fusion | flops 23706992640 | bytes 83378176 | tf_op jit(solution)/shard_map/transpose(jvp())/dot_general | solution.py:22
  593.9 44.1 %fusion.65 = bf16[1024,2816]{1,0:T(8,128)(2,1)} fusion(f32[4096,2816]{1,0:T(8,128)} %fusion.59, f32[4096,2816]{1,0:T(8,128)} %get-tuple-element.31, bf16[4096,2816]{1,0:T(8,128)(2,1)} %convolution_convert_fusion, bf16[1,4096,1024]{1,2,0:T(8,128)(2,1)} %copy.20, f32[4096]{0:T(1024)S(1)} %copy-done.13), kind=kOutput, calls=%fused_computation.97 | convolution fusion | flops 23764664320 | bytes 129515520 | tf_op jit(solution)/shard_map/transpose(jvp())/dot_general | solution.py:21
  638.1 33.1 %convolution_convert_fusion.3 = bf16[1024,2816]{1,0:T(8,128)(2,1)} fusion(bf16[4096,2816]{1,0:T(8,128)(2,1)} %get-tuple-element.34, bf16[4096,1024]{0,1:T(8,128)(2,1)} %get-tuple-element.33, f32[4096]{0:T(1024)S(1)} %copy-done.9), kind=kOutput, calls=%fused_computation.100 | convolution fusion | flops 23634903040 | bytes 37240832 | tf_op jit(solution)/shard_map/transpose(jvp())/dot_general | solution.py:21
  671.4 36.1 %reduce-scatter.7.cloned.1.call-done = bf16[256,2816]{1,0:T(8,128)(2,1)} async-done(((bf16[1024,2816]{1,0:T(8,128)(2,1)}), bf16[256,2816]{1,0:T(8,128)(2,1)}) %reduce-scatter.7.cloned.1.call-update) | async-done | bytes 1441808 | tf_op jit(solution)/shard_map/reduce_scatter | solution.py:43
  707.5 51.0 %reduce-scatter.9.cloned.1.call-done = bf16[256,2816]{1,0:T(8,128)(2,1)} async-done(((bf16[1024,2816]{1,0:T(8,128)(2,1)}), bf16[256,2816]{1,0:T(8,128)(2,1)}) %reduce-scatter.9.cloned.1.call-update) | async-done | bytes 1441808 | tf_op jit(solution)/shard_map/reduce_scatter | solution.py:43
  758.5 200.8 %all-reduce.3.cloned.1.call-done = (bf16[1,256,2816]{2,1,0:T(8,128)(2,1)}, bf16[1,256,2816]{2,1,0:T(8,128)(2,1)}, bf16[1,256,2816]{2,1,0:T(8,128)(2,1)}, bf16[1,...) async-done(((bf16[1,256,2816]{2,1,0:T(8,128)(2,1)}, bf16[1,256,2816]{2,1,0:T(8,128)(2,1)}, bf16[1,256,2816]{2,1,0:T(8,128)(2,1)}, ...) | async-done | bytes 8650768 | tf_op jit(solution)/shard_map/psum | solution.py:43
  980.5 12.1 %fusion.43 = (bf16[2,704,1024]{2,1,0:T(8,128)(2,1)}, f32[2,704,1024]{2,1,0:T(8,128)}, f32[2,704,1024]{2,1,0:T(8,128)}) fusion(bf16[2,704,1024]{2,1,0:T(8,128)(2,1)S(1)} %copy-done.3, f32[]{:T(128)S(6)} %min_shard_map.3, bf16[1,704,1024]{2,1,0:T(8,128)(2,1)} %get-tuple-element.13, bf16[1,704,1024]{2,1,0:T(8,128)(2,1)} %get-tuple-element.14, ...), kind=kLoop, calls=%fused_computation.77 | loop fusion | flops 28835840 | bytes 31719428 | tf_op jit(solution)/shard_map/convert_element_type | solution.py:30
  993.9 18.2 %fusion.34 = (bf16[2,256,2816]{2,1,0:T(8,128)(2,1)}, f32[2,256,2816]{2,1,0:T(8,128)}, f32[2,256,2816]{2,1,0:T(8,128)}, bf16[2,256,2816]{2,1,0:T(8,128)(2,1)}, f3...) fusion(bf16[2,256,2816]{2,1,0:T(8,128)(2,1)S(1)} %copy-done, f32[]{:T(128)S(6)} %min_shard_map.3, ...), kind=kLoop, calls=%fused_computation.68 | loop fusion | flops 57671680 | bytes 63438852 | tf_op jit(solution)/shard_map/convert_element_type | solution.py:30
  (76 shorter events, 62.9 us)
Async XLA Ops:
  7.2 47.3 %all-gather.13.cloned.1.call-start = ((), (), s32[]{:S(2)}) async-start(), calls=%async_computation.12 | async-start | bytes 7208960 | tf_op jit(solution)/shard_map/all_gather | solution.py:40
  11.0 86.3 %all-gather.15.cloned.1.call-start = ((), (), s32[]{:S(2)}) async-start(), calls=%async_computation.13 | async-start | bytes 7208960 | tf_op jit(solution)/shard_map/all_gather | solution.py:40
  12.8 139.3 %all-gather.17.cloned.1.call-start = ((), (), s32[]{:S(2)}) async-start(), calls=%async_computation.14 | async-start | bytes 7208960 | tf_op jit(solution)/shard_map/all_gather | solution.py:40
  16.5 168.3 %all-gather.21.cloned.1.call-start = ((), (), s32[]{:S(2)}) async-start(), calls=%async_computation.16 | async-start | bytes 7208960 | tf_op jit(solution)/shard_map/all_gather | solution.py:40
  17.1 208.0 %all-gather.23.cloned.1.call-start = ((), (), s32[]{:S(2)}) async-start(), calls=%async_computation.17 | async-start | bytes 7208960 | tf_op jit(solution)/shard_map/all_gather | solution.py:40
  17.7 250.0 %all-gather.19.cloned.1.call-start = ((), (), s32[]{:S(2)}) async-start(), calls=%async_computation.15 | async-start | bytes 7208960 | tf_op jit(solution)/shard_map/all_gather | solution.py:40
  18.3 653.0 %reduce-scatter.15.cloned.1.call-start = ((), (), s32[]{:S(2)}) async-start(), calls=%async_computation.10 | async-start | bytes 7208960 | tf_op jit(solution)/shard_map/reduce_scatter | solution.py:43
  35.4 61.9 %copy-start.12 = (f32[4096]{0:T(1024)}, f32[4096]{0:T(1024)S(1)}, u32[]{:S(2)}) copy-start(f32[4096]{0:T(1024)S(1)} %add_rsqrt_fusion) | copy-start | bytes 49156
  184.8 31.7 %copy-start.10 = (f32[4096]{0:T(1024)}, f32[4096]{0:T(1024)S(1)}, u32[]{:S(2)}) copy-start(f32[4096]{0:T(1024)S(1)} %get-tuple-element.32) | copy-start | bytes 49156
  184.8 216.4 %copy-start.8 = (f32[4096]{0:T(1024)}, f32[4096]{0:T(1024)S(1)}, u32[]{:S(2)}) copy-start(f32[4096]{0:T(1024)S(1)} %fusion.77) | copy-start | bytes 49156
  267.7 62.4 %copy-start.14 = (bf16[1,1024,2816]{2,1,0:T(8,128)(2,1)S(1)}, bf16[1,1024,2816]{2,1,0:T(8,128)(2,1)}, u32[]{:S(2)}) copy-start(bf16[1,1024,2816]{2,1,0:T(8,128)(2,1)} %all-gather.19.cloned.1.call-done) | copy-start | bytes 17301508
  358.9 42.3 %copy-start.11 = (f32[4096]{0:T(1024)S(1)}, f32[4096]{0:T(1024)}, u32[]{:S(2)}) copy-start(f32[4096]{0:T(1024)} %copy-done.10) | copy-start | bytes 49156
  448.4 223.0 %reduce-scatter.17.cloned.1.call-start = ((), (), s32[]{:S(2)}) async-start(), calls=%async_computation.11 | async-start | bytes 7208960 | tf_op jit(solution)/shard_map/reduce_scatter | solution.py:43
  489.5 30.7 %copy-start.13 = (f32[4096]{0:T(1024)S(1)}, f32[4096]{0:T(1024)}, u32[]{:S(2)}) copy-start(f32[4096]{0:T(1024)} %copy-done.12) | copy-start | bytes 49156
  489.5 181.8 %reduce-scatter.11.cloned.1.call-start = ((), (), s32[]{:S(2)}) async-start(), calls=%async_computation.8 | async-start | bytes 7208960 | tf_op jit(solution)/shard_map/reduce_scatter | solution.py:43
  520.3 36.9 %copy-start.9 = (f32[4096]{0:T(1024)S(1)}, f32[4096]{0:T(1024)}, u32[]{:S(2)}) copy-start(f32[4096]{0:T(1024)} %copy-done.8) | copy-start | bytes 49156
  557.1 114.3 %reduce-scatter.13.cloned.1.call-start = ((), (), s32[]{:S(2)}) async-start(), calls=%async_computation.9 | async-start | bytes 7208960 | tf_op jit(solution)/shard_map/reduce_scatter | solution.py:43
  593.8 113.7 %reduce-scatter.7.cloned.1.call-start = ((), (), s32[]{:S(2)}) async-start(), calls=%async_computation.6 | async-start | bytes 7208960 | tf_op jit(solution)/shard_map/reduce_scatter | solution.py:43
  638.0 120.5 %reduce-scatter.9.cloned.1.call-start = ((), (), s32[]{:S(2)}) async-start(), calls=%async_computation.7 | async-start | bytes 7208960 | tf_op jit(solution)/shard_map/reduce_scatter | solution.py:43
  671.2 288.1 %all-reduce.3.cloned.1.call-start = ((), (), s32[]{:S(2)}) async-start(), calls=%async_computation.18 | async-start | bytes 17301504 | tf_op jit(solution)/shard_map/psum | solution.py:43
  758.5 221.9 %copy-start.3 = (bf16[2,704,1024]{2,1,0:T(8,128)(2,1)S(1)}, bf16[2,704,1024]{2,1,0:T(8,128)(2,1)}, u32[]{:S(2)}) copy-start(bf16[2,704,1024]{2,1,0:T(8,128)(2,1)} %param.15) | copy-start | bytes 8650756
  980.4 12.1 %copy-start = (bf16[2,256,2816]{2,1,0:T(8,128)(2,1)S(1)}, bf16[2,256,2816]{2,1,0:T(8,128)(2,1)}, u32[]{:S(2)}) copy-start(bf16[2,256,2816]{2,1,0:T(8,128)(2,1)} %param.13) | copy-start | bytes 8650756
  980.5 12.9 %copy-start.6 = (bf16[1,256,2816]{2,1,0:T(8,128)(2,1)S(1)}, bf16[1,256,2816]{2,1,0:T(8,128)(2,1)}, u32[]{:S(2)}) copy-start(bf16[1,256,2816]{2,1,0:T(8,128)(2,1)} %get-tuple-element.11) | copy-start | bytes 4325380
  980.5 13.4 %copy-start.7 = (bf16[1,256,2816]{2,1,0:T(8,128)(2,1)S(1)}, bf16[1,256,2816]{2,1,0:T(8,128)(2,1)}, u32[]{:S(2)}) copy-start(bf16[1,256,2816]{2,1,0:T(8,128)(2,1)} %get-tuple-element.12) | copy-start | bytes 4325380
  (4 other events, 40.2 us)
Sparse Core Ops, SparseCore 0:
  11.1 43.4 all-gather.12
  56.6 40.5 all-gather.14
  99.4 40.5 all-gather.16
  141.9 40.5 all-gather.20
  184.5 40.5 all-gather.22
  227.1 40.5 all-gather.18
  448.5 48.0 reduce-scatter.14
  499.6 48.0 reduce-scatter.16
  557.2 48.0 reduce-scatter.10
  608.2 48.0 reduce-scatter.12
  659.4 48.0 reduce-scatter.6
  710.4 48.0 reduce-scatter.8
  761.4 197.8 all-reduce.2
where the time goes:
time: 1030 us; the launch traced here: 1020 us
  matrix products  573 us (56%)
  waiting for transfers between devices  327 us (32%)
  other arithmetic  60.8 us (6%)
  local copies, waits for them, and re-layouts  33.8 us (3%)
  between operations  17.2 us (2%)
    dot_general x5, matrix products, layer(): up = jnp.dot(a, w['w_up'], preferred_element_type=jnp.float32)  203 us
    dot_general x5, matrix products, layer(): gate = jnp.dot(a, w['w_gate'], preferred_element_type=jnp.float32)  201 us
    psum x1, waiting for transfers between devices, summed(): lax.psum(lax.psum_scatter(term, 's', scatter_dimension=0, tiled=True), 'r')  201 us
    dot_general x5, matrix products, matmul(): jnp.dot(a, w, preferred_element_type=jnp.float32).astype(jnp.bfloat16)  169 us
    reduce_scatter x6, waiting for transfers between devices, summed(): lax.psum_scatter(term, 's', scatter_dimension=0, tiled=True)  87.2 us
    all_gather x6, waiting for transfers between devices, fetched(): lax.all_gather(w[number], 's', axis=0, tiled=True)  36.8 us
    convert_element_type x2, other arithmetic, adamw(): return ((w - 0.02 * step).astype(jnp.bfloat16), m, v)  30.2 us
    unnamed x32, local copies, waits for them, and re-layouts  24.6 us
  transfers between devices with their start and end apart: 13, of which 7 were waited for; matrix products, arithmetic and copies ran while one was open for 43% of the time, Pallas kernels for 0%

commit v1 on v0

v1 whole, which is shorter than its diff:
```python
import functools

import jax
import jax.numpy as jnp
from jax import lax
from jax.experimental import pallas as pl
from jax.experimental.pallas import tpu as pltpu
from jax.sharding import PartitionSpec as P

MESH = pl.DeviceIdType.MESH
BF, F32 = jnp.bfloat16, jnp.float32
ANY = pl.BlockSpec(memory_space=pl.ANY)
NN = (((1,), (0,)), ((), ()))
NT = (((1,), (1,)), ((), ()))
TN = (((0,), (0,)), ((), ()))
N, D, FF = 4096, 1024, 2816
C = 256
NC = FF // C
T, S = 1024, 2
R = T // S
TRIPS = N // T


def dot(a, b, how):
    return lax.dot_general(a, b, how, preferred_element_type=F32)


def ds(start, size):
    return pl.ds(pl.multiple_of(start, size), size)


def up(v):
    return v.astype(F32)


def normed_rows(ref, row, size=64):
    def block(i, _):
        rows = ds(row + i * size, size)
        wide = up(ref[rows, :])
        scale = lax.rsqrt(jnp.mean(wide * wide, -1, keepdims=True) + 1e-6)
        ref[rows, :] = (wide * scale).astype(BF)
        return 0

    lax.fori_loop(0, T // size, block, 0)


def forward_kernel(x_hbm, wg_hbm, wu_hbm, wd_hbm, h_hbm, a_hbm, gate_hbm, up_hbm,
                   a, acc, wg, wu, wd, gt, ut, act, xt, isem, wsem, osem, hsem):
    def loads(p, slot):
        return [pltpu.make_async_copy(src.at[p], dst.at[slot], wsem.at[slot, i])
                for i, (src, dst) in enumerate(((wg_hbm, wg), (wu_hbm, wu), (wd_hbm, wd)))]

    def saves(p, t, slot):
        rows = ds(t * T, T)
        return [pltpu.make_async_copy(src.at[slot], dst.at[p, rows], osem.at[slot, i])
                for i, (src, dst) in enumerate(((gt, gate_hbm), (ut, up_hbm)))]

    xin = [pltpu.make_async_copy(x_hbm.at[pl.ds(t * T, T)], a.at[pl.ds(t * T, T)], isem.at[t]) for t in range(TRIPS)]
    for copy in xin:
        copy.start()
    for copy in loads(0, 0):
        copy.start()
    for t in range(TRIPS):
        xin[t].wait()
        normed_rows(a, t * T)
    aout = pltpu.make_async_copy(a, a_hbm, isem.at[TRIPS])
    aout.start()

    def chunk(p, _):
        w = lax.rem(p, 2)
        for copy in loads(p, w):
            copy.wait()

        @pl.when(p + 1 < NC)
        def _():
            for copy in loads(p + 1, 1 - w):
                copy.start()

        def trip(t, _):
            o = lax.rem(t, 2)

            @pl.when(p * TRIPS + t >= 2)
            def _():
                for copy in saves(0, 0, o):
                    copy.wait()

            def rows(i):
                return ds(t * T + i * R, R)

            def first(i):
                at = a[rows(i), :]
                gt[o, i * R : (i + 1) * R] = dot(at, wg[w], NN)
                ut[o, i * R : (i + 1) * R] = dot(at, wu[w], NN)

            def middle(i):
                g, u = gt[o, i * R : (i + 1) * R], ut[o, i * R : (i + 1) * R]
                act[i] = (g / (1.0 + jnp.exp(-g)) * u).astype(BF)

            def last(i):
                acc[rows(i), :] = jnp.where(p == 0, 0.0, acc[rows(i), :]) + dot(act[i], wd[w], NN)

            first(0)
            for i in range(S):
                if i + 1 < S:
                    first(i + 1)
                middle(i)
                last(i)
            for copy in saves(p, t, o):
                copy.start()

            @pl.when(p == NC - 1)
            def _():
                copy = pltpu.make_async_copy(x_hbm.at[ds(t * T, T)], xt, hsem.at[0])

                @pl.when(t > 0)
                def _():
                    pltpu.make_async_copy(a.at[ds(t * T, T)], h_hbm.at[ds(t * T, T)], hsem.at[1]).wait()

                @pl.when(t == 0)
                def _():
                    pltpu.make_async_copy(a, a_hbm, isem.at[TRIPS]).wait()

                copy.start()
                copy.wait()

                def block(i, _):
                    r = ds(i * 64, 64)
                    q = ds(t * T + i * 64, 64)
                    a[q, :] = (up(xt[r, :]) + up(acc[q, :].astype(BF))).astype(BF)
                    return 0

                lax.fori_loop(0, T // 64, block, 0)
                pltpu.make_async_copy(a.at[ds(t * T, T)], h_hbm.at[ds(t * T, T)], hsem.at[1]).start()

            return 0

        lax.fori_loop(0, TRIPS, trip, 0)
        return 0

    lax.fori_loop(0, NC, chunk, 0)
    for o in range(2):
        for copy in saves(0, 0, o):
            copy.wait()
    pltpu.make_async_copy(a.at[pl.ds(0, T)], h_hbm.at[pl.ds(0, T)], hsem.at[1]).wait()


def forward(x, wg, wu, wd):
    return pl.pallas_call(
        forward_kernel,
        name="forward0",
        in_specs=[ANY] * 4,
        out_specs=[ANY] * 4,
        out_shape=[jax.ShapeDtypeStruct((N, D), BF)] * 2 + [jax.ShapeDtypeStruct((NC, N, C), F32)] * 2,
        scratch_shapes=[
            pltpu.VMEM((N, D), BF), pltpu.VMEM((N, D), F32),
            pltpu.VMEM((2, D, C), BF), pltpu.VMEM((2, D, C), BF), pltpu.VMEM((2, C, D), BF),
            pltpu.VMEM((2, T, C), F32), pltpu.VMEM((2, T, C), F32), pltpu.VMEM((S, R, C), BF), pltpu.VMEM((T, D), BF),
            pltpu.SemaphoreType.DMA((TRIPS + 1,)), pltpu.SemaphoreType.DMA((2, 3)), pltpu.SemaphoreType.DMA((2, 2)), pltpu.SemaphoreType.DMA((2,)),
        ],
        compiler_params=pltpu.CompilerParams(vmem_limit_bytes=62 * 2**20),
    )(x, wg, wu, wd)


def backward_kernel(h_hbm, dy_hbm, wg_hbm, wu_hbm, wd_hbm, wd0_hbm, a0_hbm, gate_hbm, up_hbm,
                    gg_hbm, gu_hbm, gd_hbm, sq_ref,
                    a, dy, da, wg, wu, wd, acc_g, acc_u, acc_d, gt, ut, dt, act, dg, du,
                    send_a, recv_a, own_b, send_b, recv_b, send_c, recv_c, out,
                    isem, wsem, tsem, sa, ra, sb, rb, sc, rc, osem, dsem):
    me, mr = lax.axis_index("s"), lax.axis_index("r")
    x, c = me // 2, lax.rem(me, 2)
    sib, xn, yn = {"s": me + 1 - 2 * c}, {"s": lax.rem(me + 2, 4)}, {"r": 1 - mr}
    barrier = pltpu.get_barrier_semaphore()
    for peer in (sib, xn, yn):
        pl.semaphore_signal(barrier, inc=1, device_id=peer, device_id_type=MESH)
    pl.semaphore_wait(barrier, 3)

    def copy_a(u):
        s = lax.rem(u, 2)
        return pltpu.make_async_remote_copy(send_a, recv_a.at[s], sa, ra.at[s], device_id=sib, device_id_type=MESH)

    def copy_b(u):
        s, q = lax.rem(u, 2), lax.rem(u, 4)
        return pltpu.make_async_remote_copy(send_b.at[s], recv_b.at[q], sb.at[s], rb.at[q], device_id=xn, device_id_type=MESH)

    def copy_c(u):
        s, q = lax.rem(u, 2), lax.rem(u, 4)
        return pltpu.make_async_remote_copy(send_c.at[s], recv_c.at[q], sc.at[s], rc.at[q], device_id=yn, device_id_type=MESH)

    def part(s, m, xd, cc):
        if m < 2:
            return [(slice(0, 256), (acc_g, acc_u)[m][s, ds(512 * xd + 256 * cc, 256), :])]
        return [(slice(128 * k, 128 * k + 128), acc_d[s, ds(128 * xd, 128), ds(512 * cc + 256 * k, 256)]) for k in range(2)]

    def stage_a(u):
        s = lax.rem(u, 2)

        @pl.when(u >= 1)
        def _():
            copy_a(u - 1).wait_send()

        for xd in range(2):
            for m in range(3):
                for rows, term in part(s, m, xd, 1 - c):
                    send_a[xd, m, rows, :] = term.astype(BF)
        copy_a(u).start()

    def stage_b(u):
        s = lax.rem(u, 2)
        copy_a(u).wait_recv()

        @pl.when(u >= 2)
        def _():
            copy_b(u - 2).wait_send()

        for m in range(3):
            for rows, term in part(s, m, 1 - x, c):
                send_b[s, m, rows, :] = (term + up(recv_a[s, 1 - x, m, rows, :])).astype(BF)
        copy_b(u).start()
        for m in range(3):
            for rows, term in part(s, m, x, c):
                own_b[s, m, rows, :] = term + up(recv_a[s, x, m, rows, :])

    def stage_c(u):
        s, q = lax.rem(u, 2), lax.rem(u, 4)
        copy_b(u).wait_recv()

        @pl.when(u >= 2)
        def _():
            copy_c(u - 2).wait_send()

        send_c[s] = (own_b[s] + up(recv_b[q])).astype(BF)
        copy_c(u).start()

    def outs(u, wait):
        s, layer, p = lax.rem(u, 2), 1 - u // NC, lax.rem(u, NC)
        for m, dst in ((0, gg_hbm), (1, gu_hbm)):
            for k in range(2):
                copy = pltpu.make_async_copy(out.at[s, m, :, pl.ds(128 * k, 128)], dst.at[layer, :, ds((p + NC * k) * 128, 128)], osem.at[s, 2 * m + k])
                copy.wait() if wait else copy.start()
        for i in range(2):
            q = 2 * p + i
            owner = q // NC
            for k in range(2):
                src = out.at[s, 2, pl.ds(128 * k + 64 * i, 64), :]
                dst = gd_hbm.at[layer, ds((q - NC * owner) * 64, 64), ds(512 * c + 256 * k, 256)]
                local = pltpu.make_async_copy(src, dst, osem.at[s, 4 + 2 * i + k])
                far = pltpu.make_async_remote_copy(src, dst, osem.at[s, 4 + 2 * i + k], dsem.at[layer], device_id=sib, device_id_type=MESH)

                @pl.when(owner == c)
                def _():
                    local.wait() if wait else local.start()

                @pl.when(owner != c)
                def _():
                    far.wait_send() if wait else far.start()

    def stage_d(u):
        s, q = lax.rem(u, 2), lax.rem(u, 4)
        copy_c(u).wait_recv()

        @pl.when(u >= 2)
        def _():
            outs(u - 2, True)

        total = (up(send_c[s]) + up(recv_c[q])).astype(BF)
        out[s] = total
        wide = up(total)
        sq_ref[...] += jnp.sum((wide * wide).reshape(96, 8, 256), axis=0)
        outs(u, False)

    def comm(u, t):
        @pl.when((t == 0) & (u >= 1))
        def _():
            stage_a(u - 1)

        @pl.when((t == 0) & (u >= 4))
        def _():
            stage_d(u - 4)

        @pl.when((t == 2) & (u >= 1))
        def _():
            stage_b(u - 1)

        @pl.when((t == 3) & (u >= 2))
        def _():
            stage_c(u - 2)

    def loads(p, slot):
        return [pltpu.make_async_copy(src.at[p], dst.at[slot], wsem.at[slot, i])
                for i, (src, dst) in enumerate(((wg_hbm, wg), (wu_hbm, wu), (wd_hbm, wd)))]

    def load0(p, slot):
        return pltpu.make_async_copy(wd0_hbm.at[p], wd.at[slot], wsem.at[slot, 2])

    def saved(p, t):
        s, rows = lax.rem(t, 2), ds(t * T, T)
        return [pltpu.make_async_copy(src.at[p, rows], dst.at[s], tsem.at[s, i]) for i, (src, dst) in enumerate(((gate_hbm, gt), (up_hbm, ut)))]

    def tile(src, dst, t, k):
        return pltpu.make_async_copy(src.at[ds(t * T, T)], dst.at[ds(t * T, T)], isem.at[k, t])

    for t in range(TRIPS):
        tile(h_hbm, a, t, 0).start()
        tile(dy_hbm, dy, t, 1).start()
    for copy in loads(0, 0):
        copy.start()
    sq_ref[...] = jnp.zeros_like(sq_ref)
    for t in range(TRIPS):
        tile(h_hbm, a, t, 0).wait()
        normed_rows(a, t * T)
        tile(dy_hbm, dy, t, 1).wait()

    def pointwise(i, g, u):
        d = up(dt[i].astype(BF))
        sig = 1.0 / (1.0 + jnp.exp(-g))
        silu = g * sig
        act[i] = (silu * u).astype(BF)
        du[i] = (d * silu).astype(BF)
        dg[i] = (d * u * (sig * (1.0 + g * (1.0 - sig)))).astype(BF)

    def weight_grads(u, t):
        s, rows = lax.rem(u, 2), ds(t * T, T)
        at, dyt = a[rows, :], dy[rows, :]
        acc_g[s] = jnp.where(t == 0, 0.0, acc_g[s]) + dot(at, dg[...].reshape(T, C), TN)
        acc_u[s] = jnp.where(t == 0, 0.0, acc_u[s]) + dot(at, du[...].reshape(T, C), TN)
        acc_d[s] = jnp.where(t == 0, 0.0, acc_d[s]) + dot(act[...].reshape(T, C), dyt, TN)

    def norm_back(t):
        def block(i, _):
            rows = ds(t * T + i * 64, 64)
            wide, g = up(a[rows, :]), up(da[rows, :].astype(BF))
            scale = lax.rsqrt(jnp.mean(wide * wide, -1, keepdims=True) + 1e-6)
            inner = jnp.sum(g * wide, -1, keepdims=True) * (scale * scale * scale * (1.0 / D))
            dy[rows, :] = (up(dy[rows, :]) + up((g * scale - wide * inner).astype(BF))).astype(BF)
            return 0

        lax.fori_loop(0, T // 64, block, 0)

    def chunk1(u, _):
        w = lax.rem(u, 2)
        for copy in loads(u, w):
            copy.wait()

        @pl.when(u + 1 < NC)
        def _():
            for copy in loads(u + 1, 1 - w):
                copy.start()

        @pl.when(u + 1 == NC)
        def _():
            load0(0, 1 - w).start()

        def trip(t, _):
            comm(u, t)

            @pl.when((u == NC - 1) & (t > 0))
            def _():
                tile(h_hbm, a, t - 1, 0).wait()
                norm_back(t - 1)
                tile(a0_hbm, a, t - 1, 0).start()

            def rows(i):
                return ds(t * T + i * R, R)

            def first(i):
                at, dyt = a[rows(i), :], dy[rows(i), :]
                gt[i, :R] = dot(at, wg[w], NN)
                ut[i, :R] = dot(at, wu[w], NN)
                dt[i] = dot(dyt, wd[w], NT)

            def last(i):
                da[rows(i), :] = jnp.where(u == 0, 0.0, da[rows(i), :]) + dot(dg[i], wg[w], NT) + dot(du[i], wu[w], NT)

            first(0)
            for i in range(S):
                if i + 1 < S:
                    first(i + 1)
                pointwise(i, gt[i, :R], ut[i, :R])
                last(i)
            weight_grads(u, t)

            @pl.when(u == NC - 1)
            def _():
                tile(h_hbm, a, t, 0).start()

            return 0

        lax.fori_loop(0, TRIPS, trip, 0)
        return 0

    lax.fori_loop(0, NC, chunk1, 0)
    for copy in saved(0, 0):
        copy.start()
    tile(h_hbm, a, TRIPS - 1, 0).wait()
    norm_back(TRIPS - 1)
    tile(a0_hbm, a, TRIPS - 1, 0).start()

    def chunk0(u, _):
        w, p = lax.rem(u, 2), u - NC
        load0(p, w).wait()

        @pl.when(p + 1 < NC)
        def _():
            load0(p + 1, 1 - w).start()

        def trip(t, _):
            comm(u, t)
            o = lax.rem(t, 2)

            @pl.when(p == 0)
            def _():
                tile(a0_hbm, a, t, 0).wait()

            for copy in saved(p, t):
                copy.wait()

            @pl.when((t + 1 < TRIPS) | (p + 1 < NC))
            def _():
                more = (t + 1) // TRIPS
                for copy in saved(p + more, t + 1 - TRIPS * more):
                    copy.start()

            def rows(i):
                return ds(t * T + i * R, R)

            def first(i):
                dt[i] = dot(dy[rows(i), :], wd[w], NT)

            first(0)
            for i in range(S):
                if i + 1 < S:
                    first(i + 1)
                pointwise(i, gt[o, i * R : (i + 1) * R], ut[o, i * R : (i + 1) * R])
            weight_grads(u, t)
            return 0

        lax.fori_loop(0, TRIPS, trip, 0)
        return 0

    lax.fori_loop(NC, 2 * NC, chunk0, 0)

    L = 2 * NC - 1
    stage_a(L)
    stage_d(L - 3)
    stage_b(L)
    stage_c(L - 1)
    stage_d(L - 2)
    stage_c(L)
    stage_d(L - 1)
    stage_d(L)
    copy_a(L).wait_send()
    for u in (L - 1, L):
        copy_b(u).wait_send()
        copy_c(u).wait_send()
        outs(u, True)
    for layer in range(2):
        got = gd_hbm.at[layer, :, ds(512 * (1 - c), 512)]
        pltpu.make_async_copy(got, got, dsem.at[layer]).wait()


def backward(h, dy, wg, wu, wd, wd0, a0, gate, upw):
    dma = pltpu.SemaphoreType.DMA
    return pl.pallas_call(
        backward_kernel,
        name="backward",
        in_specs=[ANY] * 9,
        out_specs=[ANY] * 3 + [pl.BlockSpec(memory_space=pltpu.VMEM)],
        out_shape=[jax.ShapeDtypeStruct((2, 256, FF), BF)] * 2 + [jax.ShapeDtypeStruct((2, FF // 4, D), BF), jax.ShapeDtypeStruct((8, 256), F32)],
        scratch_shapes=[
            pltpu.VMEM((N, D), BF), pltpu.VMEM((N, D), BF), pltpu.VMEM((N, D), F32),
            pltpu.VMEM((2, D, C), BF), pltpu.VMEM((2, D, C), BF), pltpu.VMEM((2, C, D), BF),
            pltpu.VMEM((2, D, C), F32), pltpu.VMEM((2, D, C), F32), pltpu.VMEM((2, C, D), F32),
            pltpu.VMEM((2, T, C), F32), pltpu.VMEM((2, T, C), F32), pltpu.VMEM((S, R, C), F32),
            pltpu.VMEM((S, R, C), BF), pltpu.VMEM((S, R, C), BF), pltpu.VMEM((S, R, C), BF),
            pltpu.VMEM((2, 3, 256, 256), BF), pltpu.VMEM((2, 2, 3, 256, 256), BF), pltpu.VMEM((2, 3, 256, 256), F32),
            pltpu.VMEM((2, 3, 256, 256), BF), pltpu.VMEM((4, 3, 256, 256), BF),
            pltpu.VMEM((2, 3, 256, 256), BF), pltpu.VMEM((4, 3, 256, 256), BF), pltpu.VMEM((2, 3, 256, 256), BF),
            dma((2, TRIPS)), dma((2, 3)), dma((2, 2)),
            dma(()), dma((2,)), dma((2,)), dma((4,)), dma((2,)), dma((4,)), dma((2, 8)), dma((2,)),
        ],
        compiler_params=pltpu.CompilerParams(vmem_limit_bytes=63 * 2**20, collective_id=0, has_side_effects=True),
    )(h, dy, wg, wu, wd, wd0, a0, gate, upw)


def adamw(w, m, v, g):
    m = 0.9 * m + 0.1 * g
    v = 0.95 * v + 0.05 * g * g
    step = m * lax.rsqrt(v + 1e-8) + 0.1 * w
    return (w - 0.02 * step).astype(BF), m, v


def solution(mesh):
    def columns(w):
        whole = lax.all_gather(w, "s", axis=0, tiled=True)
        return whole.reshape(D, 2, NC, 128).transpose(2, 0, 1, 3).reshape(NC, D, C)

    def rows(w):
        whole = lax.all_gather(w, "s", axis=0, tiled=True)
        return whole.reshape(2, NC, 128, D).transpose(1, 0, 2, 3).reshape(NC, C, D)

    def step(x, dy, *arrays):
        weights, m, v = (arrays[i : i + 3] for i in (0, 3, 6))
        wg, wu, wd = ([how(w[number]) for number in range(2)] for how, w in zip((columns, columns, rows), weights))
        h, a0, gate, upw = forward(x[0], wg[0], wu[0], wd[0])
        *gradients, sq = backward(h, dy[0], wg[1], wu[1], wd[1], wd[0], a0, gate, upw)
        squares = lax.psum(jnp.sum(sq), "s")
        count = 6.0 * D * FF
        factor = jnp.minimum(1.0, 0.5 * lax.rsqrt(squares / count + 1e-30))
        new = [adamw(up(w), m, v, up(g) * factor) for w, m, v, g in zip(weights, m, v, gradients, strict=True)]
        return tuple(one[which] for which in range(3) for one in new)

    states, cut = P(("rep", "r", "s"), None, None), P(None, "s", None)
    return jax.shard_map(
        step,
        mesh=mesh,
        in_specs=(states, states) + (cut,) * 9,
        out_specs=(P("rep", "s", None),) * 9,
        check_vma=False,
    )
```

time: 1030 us -> 822 us (0.80)
  matrix products: 573 us -> 0 us
  Pallas kernels: 0 us -> 495 us
  waiting for transfers between devices: 327 us -> 139 us
  local copies, waits for them, and re-layouts: 33.8 us -> 132 us
  other arithmetic: 60.8 us -> 30.4 us
    dot_general x15 -> x0, matrix products: 573 us -> none  [the longest x5 203 us: layer(): up = jnp.dot(a, w['w_up'], preferred_element_type=jnp.float32)]
    pallas_call x0 -> x2, Pallas kernels: none -> 495 us  [the longest x1 391 us: backward(): pl.pallas_call(backward_kernel, name='backward', in_specs=[ANY] * 9, out_...]
    psum x1 -> x0, waiting for transfers between devices: 201 us -> none  [summed(): lax.psum(lax.psum_scatter(term, 's', scatter_dimension=0, tiled=True), 'r')]
    all_gather x6, waiting for transfers between devices: 36.8 us -> 139 us  [the longest x4 92.2 us: columns(): whole = lax.all_gather(w, 's', axis=0, tiled=True)]
    reduce_scatter x6 -> x0, waiting for transfers between devices: 87.2 us -> none  [summed(): lax.psum_scatter(term, 's', scatter_dimension=0, tiled=True)]
    transpose x0 -> x4, local copies, waits for them, and re-layouts: none -> 59.7 us  [columns(): return whole.reshape(D, 2, NC, 128).transpose(2, 0, 1, 3).reshape(NC, D, C)]
    reshape x0 -> x6, local copies, waits for them, and re-layouts: none -> 52.9 us  [the longest x4 40.6 us: columns(): return whole.reshape(D, 2, NC, 128).transpose(2, 0, 1, 3).reshape(NC, D, C)]
    reduce_sum x4 -> x1, other arithmetic: 16.7 us -> 1.3 us  [step(): squares = lax.psum(jnp.sum(sq), 's')]
  transfers between devices with their start and end apart: 13 -> 6, of which waited for: 7 -> 6; matrix products, arithmetic and copies ran while one was open for 43% -> 15% of each run, Pallas kernels for 0% -> 0%
where the time goes in v1:
time: 822 us; the launch traced here: 819 us
  Pallas kernels  495 us (60%)
  waiting for transfers between devices  139 us (17%)
  local copies, waits for them, and re-layouts  132 us (16%)
  other arithmetic  30.4 us (4%)
  between operations  14.9 us (2%)
    pallas_call x1, Pallas kernels, backward(): pl.pallas_call(backward_kernel, name='backward', in_specs=[ANY] * 9, out_...  391 us
    pallas_call x1, Pallas kernels, forward(): pl.pallas_call(forward_kernel, name='forward0', in_specs=[ANY] * 4, out_s...  104 us
    all_gather x4, waiting for transfers between devices, columns(): whole = lax.all_gather(w, 's', axis=0, tiled=True)  92.2 us
    transpose x4, local copies, waits for them, and re-layouts, columns(): return whole.reshape(D, 2, NC, 128).transpose(2, 0, 1, 3).reshape(NC, D, C)  59.7 us
    all_gather x2, waiting for transfers between devices, rows(): whole = lax.all_gather(w, 's', axis=0, tiled=True)  46.6 us
    reshape x4, local copies, waits for them, and re-layouts, columns(): return whole.reshape(D, 2, NC, 128).transpose(2, 0, 1, 3).reshape(NC, D, C)  40.6 us
    convert_element_type x2, other arithmetic, adamw(): return ((w - 0.02 * step).astype(BF), m, v)  29.1 us
  transfers between devices with their start and end apart: 6, of which 6 were waited for; matrix products, arithmetic and copies ran while one was open for 15% of the time, Pallas kernels for 0%

profile of v1, /device:TPU:0, one launch (start us, length us, event | category | flops | bytes accessed | tf_op | source)
XLA Modules:
  0.0 819.3 jit_solution(7175233482871309167)
XLA Ops:
  7.2 3.8 fusion.15
  12.9 2.7 copy.36
  17.4 2.6 copy.37
  24.9 29.7 %all-gather.17.cloned.1.call-done = bf16[1,2816,1024]{2,1,0:T(8,128)(2,1)} async-done(((bf16[1,704,1024]{2,1,0:T(8,128)(2,1)}), bf16[1,2816,1024]{2,1,0:T(8,128)(2,1)}) %all-gather.17.cloned.1.call-update) | async-done | bytes 5767184 | tf_op jit(solution)/shard_map/all_gather | solution.py:498
  54.6 6.2 copy.30
  60.8 37.3 %all-gather.13.cloned.1.call-done = bf16[1,1024,2816]{1,2,0:T(8,128)(2,1)} async-done(((bf16[1,256,2816]{1,2,0:T(8,128)(2,1)}), bf16[1,1024,2816]{1,2,0:T(8,128)(2,1)}) %all-gather.13.cloned.1.call-update) | async-done | bytes 5767184 | tf_op jit(solution)/shard_map/all_gather | solution.py:494
  98.1 14.9 %copy.27 = bf16[11,1024,2,128]{3,2,1,0:T(2,128)(2,1)} copy(bf16[11,1024,2,128]{1,3,0,2:T(8,128)(2,1)} %bitcast.28) | data formatting | bytes 11534336 | tf_op jit(solution)/shard_map/transpose | solution.py:495
  113.0 10.2 %reshape.55.wg_hbm = bf16[11,1024,256]{2,1,0:T(8,128)(2,1)} reshape(bf16[11,1024,2,128]{3,2,1,0:T(2,128)(2,1)} %copy.27) | data formatting | bytes 11534336 | tf_op jit(solution)/shard_map/reshape | solution.py:495
  123.2 18.4 %all-gather.15.cloned.1.call-done = bf16[1,1024,2816]{1,2,0:T(8,128)(2,1)} async-done(((bf16[1,256,2816]{1,2,0:T(8,128)(2,1)}), bf16[1,1024,2816]{1,2,0:T(8,128)(2,1)}) %all-gather.15.cloned.1.call-update) | async-done | bytes 5767184 | tf_op jit(solution)/shard_map/all_gather | solution.py:494
  141.6 14.9 %copy.29 = bf16[11,1024,2,128]{3,2,1,0:T(2,128)(2,1)} copy(bf16[11,1024,2,128]{1,3,0,2:T(8,128)(2,1)} %bitcast.29) | data formatting | bytes 11534336 | tf_op jit(solution)/shard_map/transpose | solution.py:495
  156.5 10.2 %reshape.57.wu_hbm = bf16[11,1024,256]{2,1,0:T(8,128)(2,1)} reshape(bf16[11,1024,2,128]{3,2,1,0:T(2,128)(2,1)} %copy.29) | data formatting | bytes 11534336 | tf_op jit(solution)/shard_map/reshape | solution.py:495
  166.7 18.3 %all-gather.19.cloned.1.call-done = bf16[1,1024,2816]{1,2,0:T(8,128)(2,1)} async-done(((bf16[1,256,2816]{1,2,0:T(8,128)(2,1)}), bf16[1,1024,2816]{1,2,0:T(8,128)(2,1)}) %all-gather.19.cloned.1.call-update) | async-done | bytes 5767184 | tf_op jit(solution)/shard_map/all_gather | solution.py:494
  184.9 14.9 %copy.32 = bf16[11,1024,2,128]{3,2,1,0:T(2,128)(2,1)} copy(bf16[11,1024,2,128]{1,3,0,2:T(8,128)(2,1)} %bitcast.30) | data formatting | bytes 11534336 | tf_op jit(solution)/shard_map/transpose | solution.py:495
  199.9 10.2 %reshape.61.wg_hbm = bf16[11,1024,256]{2,1,0:T(8,128)(2,1)} reshape(bf16[11,1024,2,128]{3,2,1,0:T(2,128)(2,1)} %copy.32) | data formatting | bytes 11534336 | tf_op jit(solution)/shard_map/reshape | solution.py:495
  210.0 18.2 %all-gather.21.cloned.1.call-done = bf16[1,1024,2816]{1,2,0:T(8,128)(2,1)} async-done(((bf16[1,256,2816]{1,2,0:T(8,128)(2,1)}), bf16[1,1024,2816]{1,2,0:T(8,128)(2,1)}) %all-gather.21.cloned.1.call-update) | async-done | bytes 5767184 | tf_op jit(solution)/shard_map/all_gather | solution.py:494
  228.3 14.9 %copy.34 = bf16[11,1024,2,128]{3,2,1,0:T(2,128)(2,1)} copy(bf16[11,1024,2,128]{1,3,0,2:T(8,128)(2,1)} %bitcast.31) | data formatting | bytes 11534336 | tf_op jit(solution)/shard_map/transpose | solution.py:495
  243.2 10.2 %reshape.63.wu_hbm = bf16[11,1024,256]{2,1,0:T(8,128)(2,1)} reshape(bf16[11,1024,2,128]{3,2,1,0:T(2,128)(2,1)} %copy.34) | data formatting | bytes 11534336 | tf_op jit(solution)/shard_map/reshape | solution.py:495
  253.3 16.9 %all-gather.23.cloned.1.call-done = bf16[1,2816,1024]{2,1,0:T(8,128)(2,1)} async-done(((bf16[1,704,1024]{2,1,0:T(8,128)(2,1)}), bf16[1,2816,1024]{2,1,0:T(8,128)(2,1)}) %all-gather.23.cloned.1.call-update) | async-done | bytes 5767184 | tf_op jit(solution)/shard_map/all_gather | solution.py:498
  270.3 6.2 copy.35
  276.4 103.9 %forward0.1 = (bf16[4096,1024]{1,0:T(8,128)(2,1)}, bf16[4096,1024]{1,0:T(8,128)(2,1)}, f32[11,4096,256]{2,1,0:T(8,128)}, f32[11,4096,256]{2,1,0:T(8,128)}) custom-call(bf16[4096,1024]{1,0:T(8,128)(2,1)} %bitcast.25, bf16[11,1024,256]{2,1,0:T(8,128)(2,1)} %reshape.55.wg_hbm, bf16[11,1024,256]{2,1,0:T(8,128)(2,1)} %reshape.57.wu_hbm, ...), custom_call_target="tpu_custom_call" | custom-call | tf_op jit(solution)/shard_map/forward0/pallas_call | solution.py:148
  380.3 391.1 %backward.1 = (bf16[2,256,2816]{2,1,0:T(8,128)(2,1)}, bf16[2,256,2816]{2,1,0:T(8,128)(2,1)}, bf16[2,704,1024]{2,1,0:T(8,128)(2,1)}, f32[8,256]{1,0:T(8,128)}) custom-call(bf16[4096,1024]{1,0:T(8,128)(2,1)} %get-tuple-element.17.h_hbm, bf16[4096,1024]{1,0:T(8,128)(2,1)} %bitcast.26, bf16[11,1024,256]{2,1,0:T(8,128)(2,1)} %reshape.61.wg_hbm, ...), custom_call_target="tpu_custom_call" | custom-call | tf_op jit(solution)/shard_map/backward/pallas_call | solution.py:463
  772.7 7.6 psum.7
  781.0 12.1 %fusion.8 = (bf16[2,704,1024]{2,1,0:T(8,128)(2,1)}, f32[2,704,1024]{2,1,0:T(8,128)}, f32[2,704,1024]{2,1,0:T(8,128)}) fusion(bf16[2,704,1024]{2,1,0:T(8,128)(2,1)} %param.15, f32[]{:T(128)S(6)} %min_shard_map.3, bf16[2,704,1024]{2,1,0:T(8,128)(2,1)} %get-tuple-element.24, f32[2,704,1024]{2,1,0:T(8,128)} %param.21, f32[2,704,1024]{2,1,0:T(8,128)} %param.18), kind=kLoop, calls=%fused_computation.17 | loop fusion | flops 24510464 | bytes 31719428 | tf_op jit(solution)/shard_map/convert_element_type | solution.py:489
  795.5 17.0 %fusion.2 = (bf16[2,256,2816]{2,1,0:T(8,128)(2,1)}, f32[2,256,2816]{2,1,0:T(8,128)}, f32[2,256,2816]{2,1,0:T(8,128)}, bf16[2,256,2816]{2,1,0:T(8,128)(2,1)}, f32...) fusion(bf16[2,256,2816]{2,1,0:T(8,128)(2,1)S(1)} %copy-done.1, f32[]{:T(128)S(6)} %min_shard_map.3, ...), kind=kLoop, calls=%fused_computation.11 | loop fusion | flops 49020928 | bytes 63438852 | tf_op jit(solution)/shard_map/convert_element_type | solution.py:489
  (31 shorter events, 12.1 us)
Async XLA Ops:
  7.2 3.9 copy-start
  7.2 47.4 %all-gather.17.cloned.1.call-start = ((), (), s32[]{:S(2)}) async-start(), calls=%async_computation.2 | async-start | bytes 7208960 | tf_op jit(solution)/shard_map/all_gather | solution.py:498
  11.1 87.0 %all-gather.13.cloned.1.call-start = ((), (), s32[]{:S(2)}) async-start(), calls=%async_computation | async-start | bytes 7208960 | tf_op jit(solution)/shard_map/all_gather | solution.py:494
  12.9 2.8 copy-start.2
  15.6 126.0 %all-gather.15.cloned.1.call-start = ((), (), s32[]{:S(2)}) async-start(), calls=%async_computation.1 | async-start | bytes 7208960 | tf_op jit(solution)/shard_map/all_gather | solution.py:494
  17.4 5.3 copy-start.4
  20.1 164.9 %all-gather.19.cloned.1.call-start = ((), (), s32[]{:S(2)}) async-start(), calls=%async_computation.3 | async-start | bytes 7208960 | tf_op jit(solution)/shard_map/all_gather | solution.py:494
  22.7 205.6 %all-gather.21.cloned.1.call-start = ((), (), s32[]{:S(2)}) async-start(), calls=%async_computation.4 | async-start | bytes 7208960 | tf_op jit(solution)/shard_map/all_gather | solution.py:494
  24.3 245.9 %all-gather.23.cloned.1.call-start = ((), (), s32[]{:S(2)}) async-start(), calls=%async_computation.5 | async-start | bytes 7208960 | tf_op jit(solution)/shard_map/all_gather | solution.py:498
  781.0 12.1 %copy-start.1 = (bf16[2,256,2816]{2,1,0:T(8,128)(2,1)S(1)}, bf16[2,256,2816]{2,1,0:T(8,128)(2,1)}, u32[]{:S(2)}) copy-start(bf16[2,256,2816]{2,1,0:T(8,128)(2,1)} %param.13) | copy-start | bytes 8650756
  781.0 12.1 %copy-start.3 = (bf16[2,256,2816]{2,1,0:T(8,128)(2,1)S(1)}, bf16[2,256,2816]{2,1,0:T(8,128)(2,1)}, u32[]{:S(2)}) copy-start(bf16[2,256,2816]{2,1,0:T(8,128)(2,1)} %param.14) | copy-start | bytes 8650756
  781.0 13.6 %copy-start.5 = (bf16[2,256,2816]{2,1,0:T(8,128)(2,1)S(1)}, bf16[2,256,2816]{2,1,0:T(8,128)(2,1)}, u32[]{:S(2)}) copy-start(bf16[2,256,2816]{2,1,0:T(8,128)(2,1)} %get-tuple-element.21) | copy-start | bytes 8650756
  781.0 14.4 %copy-start.6 = (bf16[2,256,2816]{2,1,0:T(8,128)(2,1)S(1)}, bf16[2,256,2816]{2,1,0:T(8,128)(2,1)}, u32[]{:S(2)}) copy-start(bf16[2,256,2816]{2,1,0:T(8,128)(2,1)} %get-tuple-element.23) | copy-start | bytes 8650756
Sparse Core Ops, SparseCore 0:
  11.2 43.4 all-gather.16
  56.7 41.3 all-gather.12
  100.2 41.3 all-gather.14
  143.5 41.3 all-gather.18
  186.9 41.3 all-gather.20
  229.6 40.5 all-gather.22

commit v2 on v0

v2 whole, which is shorter than its diff:
```python
import functools

import jax
import jax.numpy as jnp
from jax import lax
from jax.experimental import pallas as pl
from jax.experimental.pallas import tpu as pltpu
from jax.sharding import PartitionSpec as P

MESH = pl.DeviceIdType.MESH
BF, F32 = jnp.bfloat16, jnp.float32
ANY = pl.BlockSpec(memory_space=pl.ANY)
NN = (((1,), (0,)), ((), ()))
NT = (((1,), (1,)), ((), ()))
TN = (((0,), (0,)), ((), ()))
PAIR, THREE = range(2), range(3)
N, D, FF = 4096, 1024, 2816
STRIP, PART = 128, 64
C = 2 * STRIP
NC = FF // C
R = 512
T = 2 * R
TRIPS, TILES = N // T, N // R
WIDE = 4
LONG = WIDE * R
HALF = D // 2
ROWS, PB = 16, 32
EPS = 1e-6
EARLY, AT = 4, 13


def dot(a, b, how):
    return lax.dot_general(a, b, how, preferred_element_type=F32)


def ds(start, size):
    return pl.ds(pl.multiple_of(start, size), size)


def up(v):
    return v.astype(F32)


def odd(v):
    return lax.rem(v, 2)


def loop(first, last, body):
    def step(i, nothing):
        body(i)
        return nothing

    lax.fori_loop(first, last, step, 0)


def passes(count, prepare, finish, unroll):
    def step(i):
        parts = [ds((i * unroll + k) * ROWS, ROWS) for k in range(unroll)]
        ready = [prepare(rows) for rows in parts]
        for rows, value in zip(parts, ready):
            finish(rows, value)

    loop(0, count // (ROWS * unroll), step)


def before(j, u):
    return jnp.where(j == 0, TILES - 1, j - 1), jnp.where(j == 0, u - 1, u)


def scale_of(wide):
    return lax.rsqrt(jnp.mean(wide * wide, -1, keepdims=True) + EPS)


class Gather:
    def __init__(self, layer, shards, gu, wd, sems, sends, halves):
        self.layer, self.shards, self.gu, self.wd, self.halves = layer, shards, gu, wd, halves
        self.sems, self.sends = sems, sends
        self.me, self.y = lax.axis_index("s"), lax.axis_index("r")
        self.x, self.c = self.me // 2, odd(self.me)
        self.sib, self.xn = self.me + 1 - 2 * self.c, lax.rem(self.me + 2, 4)
        self.diagonal = self.xn + 1 - 2 * self.c
        self.peers = {"sib": {"s": self.sib}, "xn": {"s": self.xn}, "yn": {"r": 1 - self.y}, "diagonal": {"s": self.diagonal}}
        self.whole = (0, C)

    def far(self, src, dst, kind, where, which):
        row = kind % 5
        sem = self.sems[kind // 5].at[row if self.halves else (row + 1) // 2, where]
        return pltpu.make_async_remote_copy(src, dst, self.sends.at[kind], sem, device_id=self.peers[which], device_id_type=MESH)

    def strips(self, p, part):
        start, size = part
        for m in PAIR:
            for k in PAIR:
                yield (self.shards[m].at[self.layer, ds(start, size), ds((p + NC * k) * STRIP, STRIP)],
                       self.gu.at[p, m, ds(C * self.me + start, size), pl.ds(STRIP * k, STRIP)])

    def block(self, p, owner, part):
        start, size = part
        return self.gu.at[p, :, ds(C * owner + start, size), :]

    def owner(self, p, i):
        return (2 * p + i) // NC

    def shard_rows(self, p, i):
        return self.shards[2].at[self.layer, ds((2 * p + i - NC * self.c) * PART, PART), :]

    def rows(self, p, i, x, half=None):
        rows = ds(STRIP * x + PART * i, PART)
        return self.wd.at[p, rows, :] if half is None else self.wd.at[p, rows, ds(HALF * half, HALF)]

    def mine(self, p, i, yes, no=None):
        pl.when(self.owner(p, i) == self.c)(yes)
        if no is not None:
            pl.when(self.owner(p, i) != self.c)(no)

    def part(self, h):
        return (STRIP * h, STRIP) if self.halves else self.whole

    def half(self, h):
        return h if self.halves else None

    def issue(self, p):
        for src, dst in self.strips(p, self.part(self.y)):
            self.far(src, dst, 1, p, "xn").start()
        for src, dst in self.strips(p, self.whole):
            self.far(src, dst, 0, p, "sib").start()
        for i in PAIR:
            def send(i=i):
                src = self.shard_rows(p, i)
                self.far(src, self.rows(p, i, self.x), 5, 2 * p + i, "sib").start()
                if self.halves:
                    src = src.at[:, ds(HALF * self.y, HALF)]
                self.far(src, self.rows(p, i, self.x, self.half(self.y)), 6, 2 * p + i, "xn").start()
            self.mine(p, i, send)

    def pass_on(self, p):
        block = self.block(p, self.xn, self.part(self.y))
        self.far(block, block, 1, p, "xn").wait_recv()
        if self.halves:
            self.far(block, block, 2, p, "yn").start()
        self.far(block, block, 3, p, "sib").start()
        for i in PAIR:
            def send(i=i):
                rows = self.rows(p, i, 1 - self.x, self.half(self.y))
                self.far(rows, rows, 6, 2 * p + i, "xn").wait_recv()
                if self.halves:
                    self.far(rows, rows, 7, 2 * p + i, "yn").start()
                self.far(rows, rows, 8, 2 * p + i, "sib").start()
            self.mine(p, i, send)

    def pass_on_y(self, p):
        block = self.block(p, self.xn, self.part(1 - self.y))
        self.far(block, block, 2, p, "yn").wait_recv()
        self.far(block, block, 4, p, "sib").start()
        for i in PAIR:
            def send(i=i):
                rows = self.rows(p, i, 1 - self.x, 1 - self.y)
                self.far(rows, rows, 7, 2 * p + i, "yn").wait_recv()
                self.far(rows, rows, 9, 2 * p + i, "sib").start()
            self.mine(p, i, send)

    def arrived(self, p):
        block = self.block(p, self.sib, self.whole)
        self.far(block, block, 0, p, "sib").wait_recv()
        ways = ((3, 8, self.y), (4, 9, 1 - self.y)) if self.halves else ((3, 8, self.y),)
        for kind, _, h in ways:
            block = self.block(p, self.diagonal, self.part(h))
            self.far(block, block, kind, p, "sib").wait_recv()
        for i in PAIR:
            def wait(i=i):
                rows = self.rows(p, i, self.x)
                self.far(rows, rows, 5, 2 * p + i, "sib").wait_recv()
                for _, kind, h in ways:
                    rows = self.rows(p, i, 1 - self.x, self.half(h))
                    self.far(rows, rows, kind, 2 * p + i, "sib").wait_recv()
            pl.when(self.owner(p, i) != self.c)(wait)

    def finish(self):
        for kind in (range(10) if self.halves else (0, 1, 3, 5, 6, 8)):
            all_rows = kind in (0, 5) or not self.halves
            if kind < 5:
                block = self.gu.at[:, :, pl.ds(0, C if all_rows else STRIP), :]
            else:
                block = self.wd.at[:, pl.ds(0, PART), :] if all_rows else self.wd.at[:, pl.ds(0, PART), pl.ds(0, HALF)]
            self.far(block, block, kind, 0, "sib").wait_send()


def kernel(x_hbm, dy_hbm, w_gate, w_up, w_down,
           h_hbm, a0_hbm, gate_hbm, up_hbm, wd0_hbm, gu1_hbm, wd1_hbm, gg_hbm, gu_hbm, gd_hbm, factor_ref,
           a, da, act0, act1, sq, sqs,
           isem, osem, tsem, wsem, xsem, own, gsem0, dsem0, sends0, gsem1, dsem1, sends1, outs_sem, dsem, ra, rb, rc, sa, sb, sc, fsem, inside):
    shards = (w_gate, w_up, w_down)
    act = (act0, act1)
    g1 = Gather(1, shards, gu1_hbm, wd1_hbm, (gsem1, dsem1), sends1, False)
    me, x, c, peers = g1.me, g1.x, g1.c, g1.peers

    def move(src, dst, sem):
        return pltpu.make_async_copy(src, dst, sem)

    def first_layer(gu, wd, xt, gt, ut):
        g0 = Gather(0, shards, gu, wd, (gsem0, dsem0), sends0, True)

        def saves(p, t, slot):
            return [move(src.at[slot], dst.at[p, ds(t * LONG, LONG)], osem.at[slot, i]) for i, (src, dst) in enumerate(((gt, gate_hbm), (ut, up_hbm)))]

        def local(p, wait):
            if wait:
                block = g0.block(p, me, g0.whole)
                move(block, block, own.at[p, 2]).wait()
            else:
                for src, dst in g0.strips(p, g0.whole):
                    move(src, dst, own.at[p, 2]).start()
            for i in PAIR:
                def go(i=i):
                    copy = move(g0.shard_rows(p, i), g0.rows(p, i, x), own.at[p, i])
                    copy.wait() if wait else copy.start()
                g0.mine(p, i, go)

        def keep(p):
            return move(wd.at[p], wd0_hbm.at[p], fsem.at[3])

        xin = [move(x_hbm.at[pl.ds(t * T, T)], a.at[t], isem.at[0, t]) for t in range(TRIPS)]
        turned = [move(xt.at[odd_], a0_hbm.at[t, :, pl.ds(R * odd_, R)], isem.at[1, 2 * t + odd_]) for t in range(TRIPS) for odd_ in PAIR]
        for copy in xin:
            copy.start()
        barrier = pltpu.get_barrier_semaphore()
        for peer in peers.values():
            pl.semaphore_signal(barrier, inc=1, device_id=peer, device_id_type=MESH)
        pl.semaphore_wait(barrier, len(peers))

        def issue0(p):
            g0.issue(p)
            local(p, False)

        def issue1(p):
            g1.issue(p)

        loop(0, 2, issue0)
        for t in range(TRIPS):
            xin[t].wait()

            def put(rows, scale):
                a[t, rows, :] = (up(a[t, rows, :]) * scale).astype(BF)

            passes(T, lambda rows: scale_of(up(a[t, rows, :])), put, 8)
            for h in PAIR:
                if t >= 1:
                    turned[2 * t + h - 2].wait()
                for k in PAIR:
                    xt[h, :, C * k : C * (k + 1)] = a[t, R * h + C * k : R * h + C * (k + 1), :].T
                turned[2 * t + h].start()
            if t == 0:
                loop(2, NC, issue0)
            if t == 1:
                g0.pass_on(0)
            if t == 2:
                g0.pass_on(1)
                loop(0, NC, issue1)
        g0.pass_on_y(0)

        def down(i, j, p):
            rows = ds(j * R, R)
            da[rows, :] = jnp.where(p == 0, 0.0, da[rows, :]) + dot(act[i][...], wd[jnp.maximum(p, 0)], NN)

        def chunk(p):
            def trip(t):
                now = 2 * p + t

                @pl.when((now >= 1) & (now + 1 < NC))
                def _():
                    g0.pass_on(now + 1)

                @pl.when((now == 1) | (now >= 3) & (now <= NC))
                def _():
                    g0.pass_on_y(jnp.maximum(now - 1, 1))

                early = (2 * (now - AT) + 4) // 5

                @pl.when((now >= AT) & ((5 * early) // 2 == now - AT) & (early < EARLY))
                def _():
                    g1.pass_on(early)

                @pl.when(t == 0)
                def _():
                    local(p, True)
                    g0.arrived(p)
                    keep(p).start()

                @pl.when(now >= 2)
                def _():
                    for copy in saves(0, 0, t):
                        copy.wait()

                for i in range(WIDE):
                    part, j = pl.ds(i * R, R), WIDE * t + i
                    at = a[2 * t + i // 2, i % 2 * R : (i % 2 + 1) * R, :]
                    gt[t, part] = dot(at, gu[p, 0], NN)
                    ut[t, part] = dot(at, gu[p, 1], NN)
                    down(1 - i % 2, *before(j, p))
                    for k in range(0, R, PB):
                        g, u = gt[t, pl.ds(i * R + k, PB)], ut[t, pl.ds(i * R + k, PB)]
                        act[i % 2][k : k + PB] = (g / (1.0 + jnp.exp(-g)) * u).astype(BF)
                for copy in saves(p, t, t):
                    copy.start()

            loop(0, N // LONG, trip)

        loop(0, NC, chunk)
        down(1, TILES - 1, NC - 1)
        for copy in turned[-2:]:
            copy.wait()
        for o in PAIR:
            for copy in saves(0, 0, o):
                copy.wait()
        move(wd, wd0_hbm, fsem.at[3]).wait()
        g0.finish()

    pl.run_scoped(first_layer, pltpu.VMEM((NC, 2, D, C), BF), pltpu.VMEM((NC, C, D), BF), pltpu.VMEM((2, D, R), BF), *[pltpu.VMEM((2, LONG, C), F32)] * 2)

    def rest(dy, wgu, wd, acc_g, acc_u, acc_d, gt, ut, dt, dg0, dg1, du0, du1, ht,
             send_a, recv_a, own_b, send_b, recv_b, send_c, recv_c, out_gu, out_d):
        dg, du = (dg0, dg1), (du0, du1)

        def copy_a(u):
            return pltpu.make_async_remote_copy(send_a, recv_a.at[odd(u)], sa, ra.at[odd(u)], device_id=peers["sib"], device_id_type=MESH)

        def copy_b(u):
            s, q = odd(u), lax.rem(u, 4)
            return pltpu.make_async_remote_copy(send_b.at[s], recv_b.at[q], sb.at[s], rb.at[q], device_id=peers["xn"], device_id_type=MESH)

        def copy_c(u):
            s, q = odd(u), lax.rem(u, 4)
            return pltpu.make_async_remote_copy(send_c.at[s], recv_c.at[q], sc.at[s], rc.at[q], device_id=peers["yn"], device_id_type=MESH)

        def outs(u, wait):
            s, layer, p = odd(u), 1 - u // NC, lax.rem(u, NC)

            def go(copy, far=False):
                (copy.wait_send if far else copy.wait)() if wait else copy.start()

            for m, dst in enumerate((gg_hbm, gu_hbm)):
                for k in PAIR:
                    go(move(out_gu.at[s, m, :, pl.ds(STRIP * k, STRIP)], dst.at[layer, :, ds((p + NC * k) * STRIP, STRIP)], outs_sem.at[s, 2 * m + k]))
            for i in PAIR:
                q, sem = 2 * p + i, outs_sem.at[s, 4 + i]
                owner = g1.owner(p, i)
                src = out_d.at[s, pl.ds(PART * i, PART), :]
                dst = gd_hbm.at[layer, ds((q - NC * owner) * PART, PART), ds(HALF * c, HALF)]
                g1.mine(p, i, lambda: go(move(src, dst, sem)),
                        lambda: go(pltpu.make_async_remote_copy(src, dst, sem, dsem.at[layer], device_id=peers["sib"], device_id_type=MESH), True))

        def part(s, m, xd, cc):
            if m < 2:
                return [(pl.ds(0, C), (acc_g, acc_u)[m][s, ds(2 * C * xd + C * cc, C), :])]
            return [(pl.ds(STRIP * k, STRIP), acc_d[s, ds(STRIP * xd, STRIP), ds(HALF * cc + C * k, C)]) for k in PAIR]

        def stage_a(u):
            @pl.when(u >= 1)
            def _():
                copy_a(u - 1).wait_send()

            for xd in PAIR:
                for m in THREE:
                    for rows, term in part(odd(u), m, xd, 1 - c):
                        send_a[xd, m, rows, :] = term.astype(BF)
            copy_a(u).start()

        def stage_b(u):
            s = odd(u)
            copy_a(u).wait_recv()

            @pl.when(u >= 2)
            def _():
                copy_b(u - 2).wait_send()

            for m in THREE:
                for rows, term in part(s, m, 1 - x, c):
                    send_b[s, m, rows, :] = (term + up(recv_a[s, 1 - x, m, rows, :])).astype(BF)
            copy_b(u).start()
            for m in THREE:
                for rows, term in part(s, m, x, c):
                    own_b[s, m, rows, :] = term + up(recv_a[s, x, m, rows, :])

        def stage_c(u):
            s = odd(u)
            copy_b(u).wait_recv()

            @pl.when(u >= 2)
            def _():
                copy_c(u - 2).wait_send()

            for m in THREE:
                send_c[s, m] = (own_b[s, m] + up(recv_b[lax.rem(u, 4), m])).astype(BF)
            copy_c(u).start()

        def stage_d(u):
            s = odd(u)
            copy_c(u).wait_recv()

            @pl.when(u >= 2)
            def _():
                outs(u - 2, True)

            for m in THREE:
                total = (up(send_c[s, m]) + up(recv_c[lax.rem(u, 4), m])).astype(BF)
                if m < 2:
                    out_gu[s, m] = total
                else:
                    for k in PAIR:
                        out_d[s, :, C * k : C * (k + 1)] = total[STRIP * k : STRIP * (k + 1)]
                sq[...] += jnp.sum((up(total) * up(total)).reshape(C // 8, 8, C), axis=0)
            outs(u, False)

        def travel(u, event, when):
            for stage, lag in (((stage_c, 3),), ((stage_a, 1), (stage_d, 4)), ((stage_b, 1),))[event]:
                @pl.when(when & (u >= lag))
                def _():
                    stage(u - lag)

        def loads(p, slot, wait):
            def go(src, dst, k):
                copy = move(src, dst, wsem.at[slot, k])
                copy.wait() if wait else copy.start()

            for m in PAIR:
                for k in PAIR:
                    go(shards[m].at[1, :, ds((p + NC * k) * STRIP, STRIP)], wgu.at[slot, m, ds(C * me, C), pl.ds(STRIP * k, STRIP)], 2 * m + k)
            for k, owner in enumerate((g1.sib, g1.xn, g1.diagonal)):
                go(g1.block(p, owner, g1.whole), wgu.at[slot, :, ds(C * owner, C), :], 4 + k)
            for i in PAIR:
                there = wd.at[slot, ds(STRIP * x + PART * i, PART), :]
                g1.mine(p, i, lambda: go(g1.shard_rows(p, i), there, 7 + i), lambda: go(g1.rows(p, i, x), there, 7 + i))
            go(wd1_hbm.at[p, ds(STRIP * (1 - x), STRIP), :], wd.at[slot, ds(STRIP * (1 - x), STRIP), :], 9)

        def load0(p, slot):
            return move(wd0_hbm.at[p], wd.at[slot], wsem.at[slot, 10])

        def saved(p, t):
            s = odd(t)
            return [move(src.at[p, ds(t * T, T)], da.at[ds(s * T, T), pl.ds(C * i, C)], tsem.at[s, i]) for i, src in enumerate((gate_hbm, up_hbm))]

        def dyin(t):
            return move(dy_hbm.at[ds(t * T, T)], dy.at[ds(t * T, T)], isem.at[0, t])

        def new(t):
            return move(a0_hbm.at[t], a.at[t], isem.at[1, t])

        def tile(hbm, j, back=False):
            k = lax.rem(j, 4)
            there, here = hbm.at[ds(j * R, R)], ht.at[k]
            return move(here, there, xsem.at[1, k]) if back else move(there, here, xsem.at[0, k])

        neighbours = ("sib", "xn", "yn")
        for which in neighbours:
            pl.semaphore_signal(inside, inc=1, device_id=peers[which], device_id_type=MESH)
        for j in range(4):
            tile(x_hbm, j).start()
        g1.arrived(0)
        loads(0, 0, False)
        for t in range(TRIPS):
            dyin(t).start()
        sq[...] = jnp.zeros_like(sq)

        def output(j):
            tile(x_hbm, j).wait()
            k, t, h = lax.rem(j, 4), j // 2, odd(j)

            def sums(rows):
                value = (up(ht[k, rows, :]) + up(da[ds(j * R + rows.start, ROWS), :].astype(BF))).astype(BF)
                ht[k, rows, :] = value
                return scale_of(up(value))

            def put(rows, scale):
                a[t, ds(h * R + rows.start, ROWS), :] = (up(ht[k, rows, :]) * scale).astype(BF)

            passes(R, sums, put, 8)
            tile(h_hbm, j, True).start()

        def norm_back(j):
            tile(h_hbm, j).wait()
            k = lax.rem(j, 4)

            def parts(part):
                rows = ds(j * R + part.start, ROWS)
                return rows, up(ht[k, part, :]), up(da[rows, :].astype(BF))

            def sums(part):
                _, wide, g = parts(part)
                scale = scale_of(wide)
                return scale, jnp.sum(g * wide, -1, keepdims=True) * (scale * scale * scale * (1.0 / D))

            def put(part, value):
                rows, wide, g = parts(part)
                scale, inner = value
                dy[rows, :] = (up(dy[rows, :]) + up((g * scale - wide * inner).astype(BF))).astype(BF)

            passes(R, sums, put, 4)

            @pl.when(odd(j) == 1)
            def _():
                new(j // 2).start()

            @pl.when(j + 4 < TILES)
            def _():
                tile(h_hbm, j + 4).start()

        def pointwise(i, gate_and_up):
            for k in range(0, R, PB):
                rows = slice(k, k + PB)
                (g, u), d = gate_and_up(k), up(dt[i, rows].astype(BF))
                sig = 1.0 / (1.0 + jnp.exp(-g))
                silu = g * sig
                act[i][rows] = (silu * u).astype(BF)
                du[i][rows] = (d * silu).astype(BF)
                dg[i][rows] = (d * u * (sig + silu * (1.0 - sig))).astype(BF)

        def input_grads(i, j, u, row=None):
            w, rows = odd(u + 2), ds((j if row is None else row) * R, R)
            da[rows, :] = jnp.where(u == 0, 0.0, da[rows, :]) + dot(dg[i][...], wgu[w, 0], NT) + dot(du[i][...], wgu[w, 1], NT)

        def weight_grads(i, j, u, turned=False, block=None):
            s, k, part = odd(u + 2), j // 2 if block is None else block, slice(i * R, (i + 1) * R)
            dyt = dy[ds((2 * k + i) * R, R), :]
            at, how = (a[k, :, part], NN) if turned else (a[k, part, :], TN)
            acc_g[s] = jnp.where(j == 0, 0.0, acc_g[s]) + dot(at, dg[i][...], how)
            acc_u[s] = jnp.where(j == 0, 0.0, acc_u[s]) + dot(at, du[i][...], how)
            acc_d[s] = jnp.where(j == 0, 0.0, acc_d[s]) + dot(act[i][...], dyt, TN)

        def chunk1(u):
            w = odd(u)
            loads(u, w, True)

            @pl.when(u == NC - 1)
            def _():
                for j in range(4):
                    tile(h_hbm, j).start()

            def trip(t):
                now = 2 * u + t
                first, last = u == 0, u == NC - 1
                travel(u, 0, t == 0)
                travel(u, 1, t == 1)

                @pl.when(first)
                def _():
                    for i in range(WIDE):
                        output(WIDE * t + i)
                    for i in PAIR:
                        dyin(2 * t + i).wait()

                @pl.when(now == 2)
                def _():
                    pl.semaphore_wait(inside, len(neighbours))
                    for j in range(TILES - WIDE, TILES):
                        tile(h_hbm, j, True).wait()

                @pl.when(EARLY + now < NC)
                def _():
                    g1.pass_on(EARLY + now)

                @pl.when((t == 1) & (u + 1 < NC))
                def _():
                    g1.arrived(u + 1)
                    loads(u + 1, 1 - w, False)

                @pl.when((t == 1) & last)
                def _():
                    load0(0, 1 - w).start()
                    for j in range(WIDE - 1):
                        norm_back(j)
                    for copy in saved(0, 0):
                        copy.start()

                for i in range(WIDE):
                    j, b, part = WIDE * t + i, i % 2, slice(i % 2 * R, (i % 2 + 1) * R)
                    at, dyt = a[2 * t + i // 2, part, :], dy[ds(j * R, R), :]
                    gt[b] = dot(at, wgu[w, 0], NN)
                    ut[b] = dot(at, wgu[w, 1], NN)
                    dt[b] = dot(dyt, wd[w], NT)
                    pj, pu = before(j, u)
                    nothing = (now == 0) & (i == 0)
                    input_grads(1 - b, pj, pu, jnp.where(nothing, 0, pj))
                    weight_grads(1 - b, pj, pu, False, jnp.where(nothing, 0, pj // 2))
                    pointwise(b, lambda k: (gt[b, k : k + PB], ut[b, k : k + PB]))

                @pl.when(now == 0)
                def _():
                    for j in range(WIDE):
                        tile(h_hbm, j, True).wait()
                        tile(x_hbm, j + WIDE).start()

                travel(u, 2, t == 1)

            loop(0, N // LONG, trip)

        loop(0, NC, chunk1)
        input_grads(1, TILES - 1, NC - 1)
        weight_grads(1, TILES - 1, NC - 1)
        for j in range(WIDE - 1, TILES):
            norm_back(j)
        for ref in (act1, dg1, du1):
            ref[...] = jnp.zeros_like(ref)

        def chunk0(u):
            w, p = odd(u), u - NC
            load0(p, w).wait()

            @pl.when(p + 1 < NC)
            def _():
                load0(p + 1, 1 - w).start()

            def trip(t):
                travel(u, 0, t == 0)
                travel(u, 1, t == 1)
                travel(u, 2, t == TRIPS - 1)

                @pl.when(p == 0)
                def _():
                    new(t).wait()

                for copy in saved(p, t):
                    copy.wait()

                @pl.when((t + 1 < TRIPS) | (p + 1 < NC))
                def _():
                    more = (t + 1) // TRIPS
                    for copy in saved(p + more, t + 1 - TRIPS * more):
                        copy.start()

                for i in PAIR:
                    j = 2 * t + i
                    dt[i] = dot(dy[ds(j * R, R), :], wd[w], NT)
                    pj, pu = before(j, u)
                    weight_grads(1 - i, pj, pu, True, jnp.where((p == 0) & (j == 0), 0, pj // 2))

                    def gate_and_up(k):
                        rows = ds(odd(t) * T + i * R + k, PB)
                        return da[rows, :C], da[rows, C : 2 * C]

                    pointwise(i, gate_and_up)

            loop(0, TRIPS, trip)

        loop(NC, 2 * NC, chunk0)
        weight_grads(1, TILES - 1, 2 * NC - 1, True)

        L = 2 * NC - 1
        for stage, u in ((stage_a, L), (stage_c, L - 2), (stage_d, L - 3), (stage_b, L), (stage_c, L - 1), (stage_d, L - 2), (stage_c, L), (stage_d, L - 1), (stage_d, L)):
            stage(u)
        copy_a(L).wait_send()
        for u in (L - 1, L):
            copy_b(u).wait_send()
            copy_c(u).wait_send()
        sqs[me] = sq[:, :STRIP] + sq[:, STRIP:]
        others = [pltpu.make_async_remote_copy(sqs.at[me], sqs.at[me], fsem.at[k], dsem.at[2 + k], device_id=peers[which], device_id_type=MESH)
                  for k, which in enumerate(("sib", "xn", "diagonal"))]
        for copy in others:
            copy.start()
        g1.finish()
        for copy in others:
            copy.wait()
        mean = jnp.sum(sqs[...]) / (3.0 * 2 * D * FF)
        factor_ref[...] = jnp.full(factor_ref.shape, 1.0) * jnp.minimum(1.0, 0.5 * lax.rsqrt(jnp.full(factor_ref.shape, mean) + 1e-30))
        outs(L - 1, True)
        outs(L, True)
        for layer in PAIR:
            got = gd_hbm.at[layer, :, ds(HALF * (1 - c), HALF)]
            move(got, got, dsem.at[layer]).wait()

    piece, f = (3, C, C), pltpu.VMEM
    pl.run_scoped(
        rest,
        f((N, D), BF), f((2, 2, D, C), BF), f((2, C, D), BF),
        f((2, D, C), F32), f((2, D, C), F32), f((2, C, D), F32),
        *[f((2, R, C), F32)] * 3, *[f((R, C), BF)] * 4, f((4, R, D), BF),
        f((2,) + piece, BF), f((2, 2) + piece, BF), f((2,) + piece, F32),
        f((2,) + piece, BF), f((4,) + piece, BF), f((2,) + piece, BF), f((4,) + piece, BF), f((2, 2, C, C), BF), f((2, STRIP, HALF), BF),
    )


def gradients(x, dy, *shards):
    dma, shape = pltpu.SemaphoreType.DMA, jax.ShapeDtypeStruct
    sides = [[dma((kinds, NC)), dma((kinds, 2 * NC)), dma((10,))] for kinds in (5, 3)]
    return pl.pallas_call(
        kernel,
        name="gradients",
        in_specs=[ANY] * 5,
        out_specs=[ANY] * 10 + [pl.BlockSpec(memory_space=pltpu.VMEM)],
        out_shape=[shape((N, D), BF), shape((TRIPS, D, T), BF), shape((NC, N, C), F32), shape((NC, N, C), F32),
                   shape((NC, C, D), BF), shape((NC, 2, D, C), BF), shape((NC, C, D), BF),
                   shape((2, C, FF), BF), shape((2, C, FF), BF), shape((2, FF // 4, D), BF), shape((8, STRIP), F32)],
        scratch_shapes=[
            pltpu.VMEM((TRIPS, T, D), BF), pltpu.VMEM((N, D), F32),
            pltpu.VMEM((R, C), BF), pltpu.VMEM((R, C), BF), pltpu.VMEM((8, C), F32), pltpu.VMEM((4, 8, STRIP), F32),
            dma((2, TILES)), *[dma((2, 2))] * 2, dma((2, 11)), dma((2, 4)), dma((NC, 3)), *sides[0], *sides[1], dma((2, 6)), dma((5,)),
            dma((2,)), dma((4,)), dma((4,)), dma(()), dma((2,)), dma((2,)), dma((4,)), pltpu.SemaphoreType.REGULAR,
        ],
        compiler_params=pltpu.CompilerParams(vmem_limit_bytes=67_000_000, collective_id=0, has_side_effects=True),
    )(x, dy, *shards)[-4:]


def adamw(w, m, v, g):
    m = 0.9 * m + 0.1 * g
    v = 0.95 * v + 0.05 * g * g
    step = m * lax.rsqrt(v + 1e-8) + 0.1 * w
    return (w - 0.02 * step).astype(BF), m, v


def solution(mesh):
    def step(x, dy, *arrays):
        weights, m, v = (arrays[i : i + 3] for i in (0, 3, 6))
        *grads, factor = gradients(x[0], dy[0], *weights)
        new = [adamw(up(w), m, v, up(g) * factor[0, 0]) for w, m, v, g in zip(weights, m, v, grads, strict=True)]
        return tuple(one[which] for which in THREE for one in new)

    states, cut = P(("rep", "r", "s"), None, None), P(None, "s", None)
    return jax.shard_map(
        step,
        mesh=mesh,
        in_specs=(states, states) + (cut,) * 9,
        out_specs=(P("rep", "s", None),) * 9,
        check_vma=False,
    )
```

time: 1030 us -> 549 us (0.53); the launches traced: 1020 us -> 549 us
  matrix products: 573 us -> 0 us
  Pallas kernels: 0 us -> 515 us
  waiting for transfers between devices: 327 us -> 0 us
  other arithmetic: 60.8 us -> 27.6 us
  local copies, waits for them, and re-layouts: 33.8 us -> 5.91 us
  between operations: 17.2 us -> 0.67 us
    dot_general x15 -> x0, matrix products: 573 us -> none  [the longest x5 203 us: layer(): up = jnp.dot(a, w['w_up'], preferred_element_type=jnp.float32)]
    pallas_call x0 -> x1, Pallas kernels: none -> 515 us  [gradients(): pl.pallas_call(kernel, name='gradients', in_specs=[ANY] * 5, out_specs=[A...]
    psum x1 -> x0, waiting for transfers between devices: 201 us -> none  [summed(): lax.psum(lax.psum_scatter(term, 's', scatter_dimension=0, tiled=True), 'r')]
    reduce_scatter x6 -> x0, waiting for transfers between devices: 87.2 us -> none  [summed(): lax.psum_scatter(term, 's', scatter_dimension=0, tiled=True)]
    all_gather x6 -> x0, waiting for transfers between devices: 36.8 us -> none  [fetched(): lax.all_gather(w[number], 's', axis=0, tiled=True)]
    unnamed x32 -> x10, local copies, waits for them, and re-layouts: 24.6 us -> 4.73 us
    reduce_sum x4 -> x0, other arithmetic: 16.7 us -> none  [the longest x3 11.6 us: step(): squares = lax.psum(sum((jnp.sum(g * g) for g in gradients)), 's')]
    add_any x1 -> x0, other arithmetic: 13.8 us -> none  [normed(): wide = h.astype(jnp.float32)]
  transfers between devices with their start and end apart: 13 -> 0, of which waited for: 7 -> 0; matrix products, arithmetic and copies ran while one was open for 43% -> 0% of each run, Pallas kernels for 0% -> 0%
where the time goes in v2:
time: 549 us
  Pallas kernels  515 us (94%)
  other arithmetic  27.6 us (5%)
  local copies, waits for them, and re-layouts  5.91 us (1%)
    pallas_call x1, Pallas kernels, gradients(): pl.pallas_call(kernel, name='gradients', in_specs=[ANY] * 5, out_specs=[A...  515 us
    convert_element_type x2, other arithmetic, adamw(): return ((w - 0.02 * step).astype(BF), m, v)  27.6 us

profile of v2, /device:TPU:0, one launch (start us, length us, event | category | flops | bytes accessed | tf_op | source)
XLA Modules:
  0.0 549.1 jit_solution(5465509546452920767)
XLA Ops:
  0.6 514.9 %gradients.1 = (bf16[4096,1024]{1,0:T(8,128)(2,1)}, bf16[4,1024,1024]{2,1,0:T(8,128)(2,1)}, f32[11,4096,256]{2,1,0:T(8,128)}, f32[11,4096,256]{2,1,0:T(8,128)}, ...) custom-call(bf16[4096,1024]{1,0:T(8,128)(2,1)} %bitcast.3, ...), custom_call_target="tpu_custom_call" | custom-call | tf_op jit(solution)/shard_map/gradients/pallas_call | solution.py:684
  515.6 1.2 slice.2
  516.8 0.0 copy-start
  516.8 0.0 copy-start.1
  516.8 0.0 copy-start.2
  516.8 0.0 copy-start.3
  516.8 0.0 copy-start.4
  516.8 13.0 %fusion.8 = (bf16[2,704,1024]{2,1,0:T(8,128)(2,1)}, f32[2,704,1024]{2,1,0:T(8,128)}, f32[2,704,1024]{2,1,0:T(8,128)}) fusion(bf16[2,704,1024]{2,1,0:T(8,128)(2,1)} %w_down.1, f32[]{:T(128)} %bitcast.2, bf16[2,704,1024]{2,1,0:T(8,128)(2,1)} %get-tuple-element.16, f32[2,704,1024]{2,1,0:T(8,128)} %param.21, f32[2,704,1024]{2,1,0:T(8,128)} %param.18), kind=kLoop, calls=%fused_computation.17 | loop fusion | flops 24510464 | bytes 31719428 | tf_op jit(solution)/shard_map/convert_element_type | solution.py:706
  529.8 0.0 copy-done
  529.8 0.0 copy-done.1
  529.8 1.4 copy-done.2
  531.2 1.6 copy-done.3
  532.9 1.6 copy-done.4
  534.5 14.6 %fusion.2 = (bf16[2,256,2816]{2,1,0:T(8,128)(2,1)}, f32[2,256,2816]{2,1,0:T(8,128)}, f32[2,256,2816]{2,1,0:T(8,128)}, bf16[2,256,2816]{2,1,0:T(8,128)(2,1)}, f32...) fusion(bf16[2,256,2816]{2,1,0:T(8,128)(2,1)S(1)} %copy-done, f32[]{:T(128)} %bitcast.2, ...), kind=kLoop, calls=%fused_computation.11 | loop fusion | flops 49020928 | bytes 63438852 | tf_op jit(solution)/shard_map/convert_element_type | solution.py:706
Async XLA Ops:
  516.8 13.0 %copy-start = (bf16[2,256,2816]{2,1,0:T(8,128)(2,1)S(1)}, bf16[2,256,2816]{2,1,0:T(8,128)(2,1)}, u32[]{:S(2)}) copy-start(bf16[2,256,2816]{2,1,0:T(8,128)(2,1)} %w_gate.1) | copy-start | bytes 8650756
  516.8 13.0 %copy-start.1 = (bf16[2,256,2816]{2,1,0:T(8,128)(2,1)S(1)}, bf16[2,256,2816]{2,1,0:T(8,128)(2,1)}, u32[]{:S(2)}) copy-start(bf16[2,256,2816]{2,1,0:T(8,128)(2,1)} %w_up.1) | copy-start | bytes 8650756
  516.8 14.5 %copy-start.2 = (f32[2,256,2816]{2,1,0:T(8,128)S(1)}, f32[2,256,2816]{2,1,0:T(8,128)}, u32[]{:S(2)}) copy-start(f32[2,256,2816]{2,1,0:T(8,128)} %param.19) | copy-start | bytes 17301508
  516.8 16.1 %copy-start.3 = (f32[2,256,2816]{2,1,0:T(8,128)S(1)}, f32[2,256,2816]{2,1,0:T(8,128)}, u32[]{:S(2)}) copy-start(f32[2,256,2816]{2,1,0:T(8,128)} %param.16) | copy-start | bytes 17301508
  516.8 17.7 %copy-start.4 = (f32[2,256,2816]{2,1,0:T(8,128)S(1)}, f32[2,256,2816]{2,1,0:T(8,128)}, u32[]{:S(2)}) copy-start(f32[2,256,2816]{2,1,0:T(8,128)} %param.20) | copy-start | bytes 17301508
